TPU v7x, 64 devices: a 2x2x8 block of a 4x4x8 slice. The times are simulated.
64 devices in a mesh: data: 4 (over x, y), model: 16 (over z, core).
Axes of the slice: x: 2, y: 2, z: 8, core: 2. Of those that a mesh axis runs over, the one named last changes fastest.
The devices are a block of a 4x4x8 slice.
Arguments:
- x_tok: bfloat16 [8, 256, 5120], P('data', 'model'), parts along dimension 0
- dy_tok: bfloat16 [8, 256, 5120], P('data', 'model'), parts along dimension 0
- w_q: bfloat16 [5120, 32, 128], P(None, 'model')
- w_k: bfloat16 [5120, 8, 128], replicated
- w_v: bfloat16 [5120, 8, 128], replicated
- w_o: bfloat16 [32, 128, 5120], P('model')
Outputs:
- output 1: bfloat16 [8, 256, 5120], P('data', 'model'), parts along dimension 0
- output 2: float32 [20480, 32, 128], P('data', 'model'), parts along dimension 0
- output 3: float32 [163840, 128], P(('data', 'model')), parts along dimension 0
- output 4: float32 [163840, 128], P(('data', 'model')), parts along dimension 0
- output 5: float32 [128, 128, 5120], P(('data', 'model')), parts along dimension 0
There are 4 independent parts. A program takes and returns all parts, laid end to end along the dimension named above; an argument that names none is the same for every part.
All inputs are finite; a program needn't handle non-finite values.
Results may differ from a plain program's by a relative error of at most 0.00937.
Values are sent between devices in bfloat16 or wider.
A program may use at most 768 MiB of HBM per device.

v0:
```python
import jax
import jax.numpy as jnp
from jax import lax
from jax.sharding import PartitionSpec as P


def sub_reduce_scatter(part_sum, sub_pos, group_size, axis_size):
    hop_dist = group_size // 2
    while hop_dist >= 1:
        half_rows = part_sum.shape[0] // 2
        is_upper = (sub_pos // hop_dist) % 2 == 1
        kept_half = jnp.where(is_upper, part_sum[half_rows:], part_sum[:half_rows])
        sent_half = jnp.where(is_upper, part_sum[:half_rows], part_sum[half_rows:])
        pair_list = [(dev_id, dev_id ^ hop_dist) for dev_id in range(axis_size)]
        part_sum = kept_half + lax.ppermute(sent_half, "model", pair_list)
        hop_dist = hop_dist // 2
    return part_sum


def solution(mesh):
    model_size = mesh.shape["model"]

    def device_grads(x_loc, dy_loc, w_q, w_k, w_v, w_o):
        micro_n, tok_loc, d_model = x_loc.shape
        heads_loc, head_dim = w_q.shape[1], w_q.shape[2]
        kv_heads = w_k.shape[1]
        group_size = model_size // kv_heads
        model_idx = lax.axis_index("model")
        kv_index = model_idx // group_size
        sub_pos = model_idx % group_size
        w_k_own = lax.dynamic_index_in_dim(w_k, kv_index, axis=1, keepdims=False)
        w_v_own = lax.dynamic_index_in_dim(w_v, kv_index, axis=1, keepdims=False)
        seq_len = tok_loc * model_size
        score_scale = head_dim ** -0.5
        q_pos = lax.broadcasted_iota(jnp.int32, (seq_len, 1), 0)
        k_pos = lax.broadcasted_iota(jnp.int32, (1, seq_len), 1)
        causal_ok = q_pos >= k_pos
        dw_q = jnp.zeros((d_model, heads_loc, head_dim), jnp.float32)
        dw_k = jnp.zeros((d_model, head_dim), jnp.float32)
        dw_v = jnp.zeros((d_model, head_dim), jnp.float32)
        dw_o = jnp.zeros((heads_loc, head_dim, d_model), jnp.float32)
        dx_list = []
        for micro_idx in range(micro_n):
            x_full = lax.all_gather(x_loc[micro_idx], "model", axis=0, tiled=True)
            dy_full = lax.all_gather(dy_loc[micro_idx], "model", axis=0, tiled=True)
            q_heads = jnp.einsum("sc,che->she", x_full, w_q, preferred_element_type=jnp.float32).astype(jnp.bfloat16)
            k_head = jnp.dot(x_full, w_k_own, preferred_element_type=jnp.float32).astype(jnp.bfloat16)
            v_head = jnp.dot(x_full, w_v_own, preferred_element_type=jnp.float32).astype(jnp.bfloat16)
            scores = jnp.einsum("qhe,ke->hqk", q_heads, k_head, preferred_element_type=jnp.float32) * score_scale
            scores = jnp.where(causal_ok, scores, -jnp.inf)
            prob_f32 = jax.nn.softmax(scores, axis=-1)
            prob_b16 = prob_f32.astype(jnp.bfloat16)
            attn_out = jnp.einsum("hqk,ke->qhe", prob_b16, v_head, preferred_element_type=jnp.float32).astype(jnp.bfloat16)
            d_out = jnp.einsum("sc,hec->she", dy_full, w_o, preferred_element_type=jnp.float32).astype(jnp.bfloat16)
            dw_o = dw_o + jnp.einsum("she,sc->hec", attn_out, dy_full, preferred_element_type=jnp.float32)
            d_prob = jnp.einsum("qhe,ke->hqk", d_out, v_head, preferred_element_type=jnp.float32)
            row_delta = jnp.einsum("qhe,qhe->hq", d_out, attn_out, preferred_element_type=jnp.float32)
            d_score = (prob_f32 * (d_prob - row_delta[:, :, None])).astype(jnp.bfloat16)
            d_q = (jnp.einsum("hqk,ke->qhe", d_score, k_head, preferred_element_type=jnp.float32) * score_scale).astype(jnp.bfloat16)
            d_k = (jnp.einsum("hqk,qhe->ke", d_score, q_heads, preferred_element_type=jnp.float32) * score_scale).astype(jnp.bfloat16)
            d_v = jnp.einsum("hqk,qhe->ke", prob_b16, d_out, preferred_element_type=jnp.float32).astype(jnp.bfloat16)
            dw_q = dw_q + jnp.einsum("sc,she->che", x_full, d_q, preferred_element_type=jnp.float32)
            dw_k = dw_k + jnp.einsum("sc,se->ce", x_full, d_k, preferred_element_type=jnp.float32)
            dw_v = dw_v + jnp.einsum("sc,se->ce", x_full, d_v, preferred_element_type=jnp.float32)
            dx_part = (jnp.einsum("she,che->sc", d_q, w_q, preferred_element_type=jnp.float32)
                       + jnp.einsum("se,ce->sc", d_k, w_k_own, preferred_element_type=jnp.float32)
                       + jnp.einsum("se,ce->sc", d_v, w_v_own, preferred_element_type=jnp.float32))
            dx_own = lax.psum_scatter(dx_part, "model", scatter_dimension=0, tiled=True)
            dx_list.append(dx_own.astype(jnp.bfloat16))
        dw_k_rows = sub_reduce_scatter(dw_k, sub_pos, group_size, model_size)
        dw_v_rows = sub_reduce_scatter(dw_v, sub_pos, group_size, model_size)
        return jnp.stack(dx_list), dw_q, dw_k_rows, dw_v_rows, dw_o

    return jax.shard_map(
        device_grads, mesh=mesh,
        in_specs=(P("data", "model", None), P("data", "model", None), P(None, "model", None),
                  P(None, None, None), P(None, None, None), P("model", None, None)),
        out_specs=(P("data", "model", None), P("data", "model", None), P(("data", "model"), None),
                   P(("data", "model"), None), P(("data", "model"), None, None)),
        check_vma=False)
```

profile of v0, /device:TPU:22, one launch (start us, length us, event | category | flops | bytes accessed | tf_op | source)
XLA Modules:
  0.0 296.1 jit_solution(3171858434485184614)
XLA Ops:
  12.6 6.5 %constant_dynamic-slice_fusion.1 = bf16[5120,1,128]{2,1,0:T(2,128)(2,1)S(1)} fusion(bf16[5120,8,128]{2,1,0:T(8,128)(2,1)} %param.9, s32[]{:T(128)S(6)} %select_n.52), kind=kLoop, calls=%fused_computation.120 | loop fusion | bytes 2621444 | tf_op jit(solution)/shard_map/jit(dynamic_index_in_dim)/dynamic_slice | solution.py:31
  20.4 6.5 %constant_dynamic-slice_fusion = bf16[5120,1,128]{2,1,0:T(2,128)(2,1)S(1)} fusion(bf16[5120,8,128]{2,1,0:T(8,128)(2,1)} %param.10, s32[]{:T(128)S(6)} %select_n.52), kind=kLoop, calls=%fused_computation.119 | loop fusion | bytes 2621444 | tf_op jit(solution)/shard_map/jit(dynamic_index_in_dim)/dynamic_slice | solution.py:32
  28.1 22.5 %all-gather.15.cloned.1.call-done = bf16[1,256,5120]{2,1,0:T(8,128)(2,1)} async-done(((bf16[1,16,5120]{2,1,0:T(8,128)(2,1)}), bf16[1,256,5120]{2,1,0:T(8,128)(2,1)}) %all-gather.15.cloned.1.call-update) | async-done | bytes 2621456 | tf_op jit(solution)/shard_map/all_gather | solution.py:45
  50.6 4.1 %bitcast_convert_fusion = (f32[2,256,128]{2,1,0:T(8,128)S(1)}, bf16[256,2,128]{2,0,1:T(8,128)(2,1)}) fusion(bf16[2,128,5120]{2,1,0:T(8,128)(2,1)} %param.11, bf16[1,256,5120]{2,1,0:T(8,128)(2,1)} %all-gather.15.cloned.1.call-done), kind=kOutput, calls=%fused_computation.113 | convolution fusion | flops 671219712 | bytes 5636096 | tf_op jit(solution)/shard_map/sc,hec->she/dot_general | solution.py:54
  54.8 33.1 %all-gather.13.cloned.1.call-done = bf16[1,256,5120]{2,1,0:T(8,128)(2,1)} async-done(((bf16[1,16,5120]{2,1,0:T(8,128)(2,1)}), bf16[1,256,5120]{2,1,0:T(8,128)(2,1)}) %all-gather.13.cloned.1.call-update) | async-done | bytes 2621456 | tf_op jit(solution)/shard_map/all_gather | solution.py:44
  87.9 3.3 %fusion.92 = bf16[128,256,1]{1,0,2:T(8,128)(2,1)S(1)} fusion(bf16[5120,128]{1,0:T(8,128)(2,1)} %bitcast.222, bf16[1,256,5120]{2,1,0:T(8,128)(2,1)} %all-gather.13.cloned.1.call-done), kind=kOutput, calls=%fused_computation.98 | convolution fusion | flops 335577088 | bytes 3997696 | tf_op jit(solution)/shard_map/dot_general | solution.py:47
  96.1 3.2 %fusion.89 = bf16[128,256,1]{1,0,2:T(8,128)(2,1)S(1)} fusion(bf16[5120,128]{1,0:T(8,128)(2,1)} %bitcast.226, bf16[1,256,5120]{2,1,0:T(8,128)(2,1)} %all-gather.13.cloned.1.call-done), kind=kOutput, calls=%fused_computation.97 | convolution fusion | flops 335577088 | bytes 3997696 | tf_op jit(solution)/shard_map/dot_general | solution.py:48
  102.8 3.2 %convolution_add_fusion.2 = f32[256,5120]{1,0:T(8,128)} fusion(f32[256,5120]{1,0:T(8,128)S(1)} %convolution_add_fusion.3, bf16[256,128]{1,0:T(8,128)(2,1)S(1)} %fusion.76, bf16[5120,128]{1,0:T(8,128)(2,1)S(1)} %bitcast.228), kind=kOutput, calls=%fused_computation.4 | convolution fusion | flops 336855040 | bytes 11862016 | tf_op jit(solution)/shard_map/se,ce->sc/dot_general | solution.py:67
  106.3 18.3 %all-gather.11.cloned.1.call-done = bf16[1,256,5120]{2,1,0:T(8,128)(2,1)} async-done(((bf16[1,16,5120]{2,1,0:T(8,128)(2,1)}), bf16[1,256,5120]{2,1,0:T(8,128)(2,1)}) %all-gather.11.cloned.1.call-update) | async-done | bytes 2621456 | tf_op jit(solution)/shard_map/all_gather | solution.py:45
  124.7 4.1 %bitcast_convert_fusion.1 = (f32[2,256,128]{2,1,0:T(8,128)}, bf16[256,2,128]{2,0,1:T(8,128)(2,1)S(1)}) fusion(bf16[2,128,5120]{2,1,0:T(8,128)(2,1)} %param.11, bf16[1,256,5120]{2,1,0:T(8,128)(2,1)} %all-gather.11.cloned.1.call-done), kind=kOutput, calls=%fused_computation.114 | convolution fusion | flops 671219712 | bytes 5636096 | tf_op jit(solution)/shard_map/sc,hec->she/dot_general | solution.py:54
  129.9 32.0 %all-gather.9.cloned.1.call-done = bf16[1,256,5120]{2,1,0:T(8,128)(2,1)} async-done(((bf16[1,16,5120]{2,1,0:T(8,128)(2,1)}), bf16[1,256,5120]{2,1,0:T(8,128)(2,1)}) %all-gather.9.cloned.1.call-update) | async-done | bytes 2621456 | tf_op jit(solution)/shard_map/all_gather | solution.py:44
  161.9 3.3 %fusion.98 = bf16[128,256,1]{1,0,2:T(8,128)(2,1)S(1)} fusion(bf16[5120,128]{1,0:T(8,128)(2,1)} %bitcast.223, bf16[1,256,5120]{2,1,0:T(8,128)(2,1)} %all-gather.9.cloned.1.call-done), kind=kOutput, calls=%fused_computation.100 | convolution fusion | flops 335577088 | bytes 3997696 | tf_op jit(solution)/shard_map/dot_general | solution.py:47
  170.2 3.2 %fusion.95 = bf16[128,256,1]{1,0,2:T(8,128)(2,1)S(1)} fusion(bf16[5120,128]{1,0:T(8,128)(2,1)} %bitcast.227, bf16[1,256,5120]{2,1,0:T(8,128)(2,1)} %all-gather.9.cloned.1.call-done), kind=kOutput, calls=%fused_computation.99 | convolution fusion | flops 335577088 | bytes 3997696 | tf_op jit(solution)/shard_map/dot_general | solution.py:48
  176.9 3.3 %convolution_add_fusion.4 = f32[256,5120]{1,0:T(8,128)} fusion(f32[256,5120]{1,0:T(8,128)S(1)} %convolution_add_fusion.5, bf16[256,128]{1,0:T(8,128)(2,1)S(1)} %fusion.75, bf16[5120,128]{1,0:T(8,128)(2,1)S(1)} %bitcast.229), kind=kOutput, calls=%fused_computation.6 | convolution fusion | flops 336855040 | bytes 11862016 | tf_op jit(solution)/shard_map/se,ce->sc/dot_general | solution.py:67
  180.3 2.4 fusion.29
  190.2 3.4 %fusion.2 = f32[5120,2,128]{0,2,1:T(8,128)} fusion(f32[2,128,5120]{2,1,0:T(8,128)S(1)} %fusion.21, bf16[256,2,128]{0,2,1:T(8,128)(2,1)S(1)} %fusion.69, bf16[1,256,5120]{2,1,0:T(8,128)(2,1)S(1)} %copy-done.3), kind=kOutput, calls=%fused_computation.8 | convolution fusion | flops 672399360 | bytes 13238272 | tf_op jit(solution)/shard_map/sc,she->che/dot_general | solution.py:62
  193.6 8.8 %copy.44 = f32[5120,2,128]{2,1,0:T(2,128)} copy(f32[5120,2,128]{0,2,1:T(8,128)} %fusion.2) | data formatting | bytes 10485760
  204.1 3.3 %convolution_add_fusion = f32[2,128,5120]{2,1,0:T(8,128)} fusion(f32[2,128,5120]{2,1,0:T(8,128)S(1)} %fusion.17, bf16[1,256,5120]{2,1,0:T(8,128)(2,1)S(1)} %copy-done.13, bf16[128,2,256]{2,0,1:T(8,128)(2,1)S(1)} %get-tuple-element.24), kind=kOutput, calls=%fused_computation.2 | convolution fusion | flops 672399360 | bytes 13238272 | tf_op jit(solution)/shard_map/she,sc->hec/dot_general | solution.py:55
  207.4 2.6 select_add_fusion.1
  210.0 2.8 copy.45
  212.7 3.5 %select_add_fusion = f32[2560,128]{0,1:T(8,128)} fusion(f32[2560,128]{0,1:T(8,128)} %collective-permute-done.1, f32[5120,128]{0,1:T(8,128)} %copy-done.12, pred[]{:T(512)S(6)} %eq.8), kind=kLoop, calls=%fused_computation.49 | loop fusion | flops 655360 | bytes 5242881 | tf_op jit(solution)/shard_map/add | solution.py:15
  216.3 2.8 copy.46
  219.0 5.6 %reduce-scatter.5.cloned.1.call-done = f32[16,5120]{1,0:T(8,128)} async-done(((f32[256,5120]{1,0:T(8,128)}), f32[16,5120]{1,0:T(8,128)}) %reduce-scatter.5.cloned.1.call-update) | async-done | bytes 327696 | tf_op jit(solution)/shard_map/reduce_scatter | solution.py:68
  225.7 61.9 %reduce-scatter.3.cloned.1.call-done = f32[16,5120]{1,0:T(8,128)} async-done(((f32[256,5120]{1,0:T(8,128)}), f32[16,5120]{1,0:T(8,128)}) %reduce-scatter.3.cloned.1.call-update) | async-done | bytes 327696 | tf_op jit(solution)/shard_map/reduce_scatter | solution.py:68
  (103 shorter events, 38.1 us)
Async XLA Ops:
  7.2 84.0 %copy-start = (bf16[5120,2,128]{2,1,0:T(2,128)(2,1)S(1)}, bf16[5120,2,128]{2,1,0:T(2,128)(2,1)}, u32[]{:S(2)}) copy-start(bf16[5120,2,128]{2,1,0:T(2,128)(2,1)} %param.8) | copy-start | bytes 7864324
  7.2 43.4 %all-gather.15.cloned.1.call-start = ((), (), s32[]{:S(2)}) async-start(), calls=%async_computation.7 | async-start | bytes 2785280 | tf_op jit(solution)/shard_map/all_gather | solution.py:45
  9.2 78.7 %all-gather.13.cloned.1.call-start = ((), (), s32[]{:S(2)}) async-start(), calls=%async_computation.6 | async-start | bytes 2785280 | tf_op jit(solution)/shard_map/all_gather | solution.py:44
  11.1 113.6 %all-gather.11.cloned.1.call-start = ((), (), s32[]{:S(2)}) async-start(), calls=%async_computation.5 | async-start | bytes 2785280 | tf_op jit(solution)/shard_map/all_gather | solution.py:45
  11.9 150.0 %all-gather.9.cloned.1.call-start = ((), (), s32[]{:S(2)}) async-start(), calls=%async_computation.4 | async-start | bytes 2785280 | tf_op jit(solution)/shard_map/all_gather | solution.py:44
  12.5 212.2 %reduce-scatter.5.cloned.1.call-start = ((), (), s32[]{:S(2)}) async-start(), calls=%async_computation.3 | async-start | bytes 5570560 | tf_op jit(solution)/shard_map/reduce_scatter | solution.py:68
  28.1 64.7 %copy-start.23 = (pred[256,256]{0,1:T(8,128)(4,1)}, pred[256,256]{0,1:T(8,128)(4,1)S(1)}, u32[]{:S(2)}) copy-start(pred[256,256]{0,1:T(8,128)(4,1)S(1)} %iota_compare_fusion) | copy-start | bytes 196612
  87.9 3.3 %copy-start.2 = (bf16[1,256,5120]{2,1,0:T(8,128)(2,1)S(1)}, bf16[1,256,5120]{2,1,0:T(8,128)(2,1)}, u32[]{:S(2)}) copy-start(bf16[1,256,5120]{2,1,0:T(8,128)(2,1)} %all-gather.13.cloned.1.call-done) | copy-start | bytes 7864324
  94.9 4.6 %copy-start.20 = (bf16[256,2,128]{2,0,1:T(8,128)(2,1)S(1)}, bf16[256,2,128]{2,0,1:T(8,128)(2,1)}, u32[]{:S(2)}) copy-start(bf16[256,2,128]{2,0,1:T(8,128)(2,1)} %get-tuple-element.20) | copy-start | bytes 393220
  94.9 4.6 %copy-start.17 = (f32[2,256,256]{1,2,0:T(8,128)S(1)}, f32[2,256,256]{1,2,0:T(8,128)}, u32[]{:S(2)}) copy-start(f32[2,256,256]{1,2,0:T(8,128)} %copy-done.16) | copy-start | bytes 1572868
  96.1 3.7 %copy-start.22 = (bf16[256,2,128]{2,0,1:T(8,128)(2,1)S(1)}, bf16[256,2,128]{2,0,1:T(8,128)(2,1)}, u32[]{:S(2)}) copy-start(bf16[256,2,128]{2,0,1:T(8,128)(2,1)} %fusion.61) | copy-start | bytes 393220
  106.1 181.4 %reduce-scatter.3.cloned.1.call-start = ((), (), s32[]{:S(2)}) async-start(), calls=%async_computation.2 | async-start | bytes 5570560 | tf_op jit(solution)/shard_map/reduce_scatter | solution.py:68
  128.8 41.2 %copy-start.18 = (bf16[256,2,128]{2,0,1:T(8,128)(2,1)}, bf16[256,2,128]{2,0,1:T(8,128)(2,1)S(1)}, u32[]{:S(2)}) copy-start(bf16[256,2,128]{2,0,1:T(8,128)(2,1)S(1)} %get-tuple-element.26) | copy-start | bytes 393220
  161.9 3.3 %copy-start.4 = (bf16[1,256,5120]{2,1,0:T(8,128)(2,1)S(1)}, bf16[1,256,5120]{2,1,0:T(8,128)(2,1)}, u32[]{:S(2)}) copy-start(bf16[1,256,5120]{2,1,0:T(8,128)(2,1)} %all-gather.9.cloned.1.call-done) | copy-start | bytes 7864324
  169.9 3.7 %copy-start.15 = (f32[2,256,256]{1,2,0:T(8,128)S(1)}, f32[2,256,256]{1,2,0:T(8,128)}, u32[]{:S(2)}) copy-start(f32[2,256,256]{1,2,0:T(8,128)} %get-tuple-element.28) | copy-start | bytes 1572868
  170.2 3.4 %copy-start.19 = (bf16[256,2,128]{2,0,1:T(8,128)(2,1)S(1)}, bf16[256,2,128]{2,0,1:T(8,128)(2,1)}, u32[]{:S(2)}) copy-start(bf16[256,2,128]{2,0,1:T(8,128)(2,1)} %copy-done.18) | copy-start | bytes 393220
  170.2 3.7 %copy-start.21 = (bf16[256,2,128]{2,0,1:T(8,128)(2,1)S(1)}, bf16[256,2,128]{2,0,1:T(8,128)(2,1)}, u32[]{:S(2)}) copy-start(bf16[256,2,128]{2,0,1:T(8,128)(2,1)} %fusion.53) | copy-start | bytes 393220
  183.4 3.7 %copy-start.10 = (f32[5120,128]{0,1:T(8,128)}, f32[5120,128]{0,1:T(8,128)S(1)}, u32[]{:S(2)}) copy-start(f32[5120,128]{0,1:T(8,128)S(1)} %fusion.4) | copy-start | bytes 7864324
  183.4 3.2 %copy-start.5 = (bf16[1,256,5120]{2,1,0:T(8,128)(2,1)S(1)}, bf16[1,256,5120]{2,1,0:T(8,128)(2,1)}, u32[]{:S(2)}) copy-start(bf16[1,256,5120]{2,1,0:T(8,128)(2,1)} %all-gather.9.cloned.1.call-done) | copy-start | bytes 7864324
  184.6 22.7 %collective-permute-start = (f32[2560,128]{0,1:T(8,128)}, f32[2560,128]{0,1:T(8,128)}, u32[]{:S(2)}, u32[]{:S(2)}) collective-permute-start(f32[2560,128]{0,1:T(8,128)} %slice_select_fusion.1), channel_id=1, source_target_pairs={{0,1},{1,0},{2,3},{3,2},{4,5},{5,4},{6,7},{7,6},{8,9},{9,8},{10,11... | collective-permute-start | bytes 3932168 | tf_op jit(solution)/shard_map/ppermute | solution.py:15
  189.1 23.6 %collective-permute-start.1 = (f32[2560,128]{0,1:T(8,128)}, f32[2560,128]{0,1:T(8,128)}, u32[]{:S(2)}, u32[]{:S(2)}) collective-permute-start(f32[2560,128]{0,1:T(8,128)} %slice_select_fusion), channel_id=1, source_target_pairs={{0,1},{1,0},{2,3},{3,2},{4,5},{5,4},{6,7},{7,6},{8,9},{9,8},{10,11... | collective-permute-start | bytes 3932168 | tf_op jit(solution)/shard_map/ppermute | solution.py:15
  193.6 8.8 %copy-start.14 = (bf16[1,256,5120]{2,1,0:T(8,128)(2,1)S(1)}, bf16[1,256,5120]{2,1,0:T(8,128)(2,1)}, u32[]{:S(2)}) copy-start(bf16[1,256,5120]{2,1,0:T(8,128)(2,1)} %all-gather.11.cloned.1.call-done) | copy-start | bytes 7864324
  204.1 3.3 %copy-start.11 = (f32[5120,128]{0,1:T(8,128)S(1)}, f32[5120,128]{0,1:T(8,128)}, u32[]{:S(2)}) copy-start(f32[5120,128]{0,1:T(8,128)} %copy-done.10) | copy-start | bytes 7864324
  212.7 76.5 %copy-start.1 = (bf16[5120,2,128]{2,1,0:T(2,128)(2,1)S(1)}, bf16[5120,2,128]{2,1,0:T(2,128)(2,1)}, u32[]{:S(2)}) copy-start(bf16[5120,2,128]{2,1,0:T(2,128)(2,1)} %param.8) | copy-start | bytes 7864324
  (9 other events, 14.4 us)
Sparse Core Ops, SparseCore 0:
  10.2 40.2 all-gather.14
  52.8 35.0 all-gather.12
  89.5 35.0 all-gather.10
  126.7 35.1 all-gather.8
  164.1 60.5 reduce-scatter.4
  226.9 60.5 reduce-scatter.2
where the time goes:
time: 297 us; the launch traced here: 296 us
  waiting for transfers between devices  175 us (59%)
  matrix products  53.2 us (18%)
  local copies, waits for them, and re-layouts  39.9 us (13%)
  between operations  14.6 us (5%)
  other arithmetic  12.5 us (4%)
    reduce_scatter x2, waiting for transfers between devices, device_grads(): dx_own = lax.psum_scatter(dx_part, 'model', scatter_dimension=0, tiled=True)  67.5 us
    all_gather x2, waiting for transfers between devices, device_grads(): x_full = lax.all_gather(x_loc[micro_idx], 'model', axis=0, tiled=True)  65.1 us
    all_gather x2, waiting for transfers between devices, device_grads(): dy_full = lax.all_gather(dy_loc[micro_idx], 'model', axis=0, tiled=True)  40.8 us
    unnamed x57, local copies, waits for them, and re-layouts  23.3 us
    dot_general x2, matrix products, device_grads(): jnp.einsum('sc,hec->she', dy_full, w_o, preferred_element_type=jnp.float32)  8.18 us
    dot_general x2, matrix products, device_grads(): jnp.dot(x_full, w_k_own, preferred_element_type=jnp.float32)  6.58 us
    dynamic_slice x1, local copies, waits for them, and re-layouts, device_grads(): w_k_own = lax.dynamic_index_in_dim(w_k, kv_index, axis=1, keepdims=False)  6.51 us
    dynamic_slice x1, local copies, waits for them, and re-layouts, device_grads(): w_v_own = lax.dynamic_index_in_dim(w_v, kv_index, axis=1, keepdims=False)  6.5 us
  transfers between devices with their start and end apart: 8, of which 6 were waited for; matrix products, arithmetic and copies ran while one was open for 33% of the time, Pallas kernels for 0%

commit v1 on v0

v1 whole, which is shorter than its diff:
```python
import functools

import jax
import jax.numpy as jnp
from jax import lax
from jax.experimental import pallas as pl
from jax.experimental.pallas import tpu as pltpu
from jax.sharding import PartitionSpec as P

BF16 = jnp.bfloat16
F32 = jnp.float32
MESH = pl.DeviceIdType.MESH

NT = (((1,), (1,)), ((), ()))
NN = (((1,), (0,)), ((), ()))
TN = (((0,), (0,)), ((), ()))


def dot(a, b, dims=NN):
    return lax.dot_general(a, b, dims, preferred_element_type=F32)


def attn_kernel(n_dev, kv_heads, x_in, dy_in, wq_in, wk_in, wv_in, wo_in,
                dx_out, xf_out, dyf_out, dq_out, dkv_out, o_out,
                xb, dyb, wq, wo, wkv, stage_q, stage_kv, unpacked,
                acc_q, acc_kv, acc_do, qb, kvb, dob, ob, dqb, dkvp, prob_b, ds_b,
                dkv_f, dkv_peer, dkv_tot,
                dx_f, dx_tmp, psend, precv, sbuf, rbuf, dx_own,
                own_sem, w_sem, kvw_sem, out_sem,
                ag_send, ag_recv, d2d_send, d2d_recv, wx_sem,
                dkv_sem, ps_send, ps_recv, rs_send, rs_recv):
    n_chip = n_dev // 2
    half = n_chip // 2
    micro_n, tok, d_model = x_in.shape
    head_dim = wk_in.shape[1]
    heads = wq.shape[1] // head_dim
    n_rows = n_dev * tok
    par_rows = n_rows // 2
    me = lax.axis_index("model")
    z, c = me // 2, me % 2
    right = lax.rem(me + 2, n_dev)
    left = lax.rem(me + n_dev - 2, n_dev)
    peer = z * 2 + (1 - c)
    scale = head_dim ** -0.5

    def to(dev):
        return {"model": dev}

    bufs = ((x_in, xb), (dy_in, dyb))
    my_row = pl.multiple_of(c * par_rows + z * tok, tok)
    own = []
    for m in range(micro_n):
        for t, (src, buf) in enumerate(bufs):
            cp = pltpu.make_async_copy(src.at[m], buf.at[m, pl.ds(my_row, tok)], own_sem.at[m, t])
            cp.start()
            own.append(cp)
    wq_cp = pltpu.make_async_copy(wq_in, stage_q, w_sem.at[0])
    wq_cp.start()
    wo_cp = pltpu.make_async_copy(wo_in, wo, w_sem.at[1])
    wo_cp.start()
    kv_rows = stage_kv.shape[1]
    n_kv = wk_in.shape[0] // kv_rows

    def kv_load(i):
        @pl.when(c == 0)
        def _():
            pltpu.make_async_copy(wk_in.at[pl.ds(i * kv_rows, kv_rows)], stage_kv.at[i % 2], kvw_sem.at[i % 2]).start()

        @pl.when(c == 1)
        def _():
            pltpu.make_async_copy(wv_in.at[pl.ds(i * kv_rows, kv_rows)], stage_kv.at[i % 2], kvw_sem.at[i % 2]).start()

    kv_load(0)
    kv_load(1)

    barrier = pltpu.get_barrier_semaphore()
    for dev in (left, right, peer):
        pl.semaphore_signal(barrier, inc=1, device_id=to(dev), device_id_type=MESH)
    pl.semaphore_wait(barrier, 3)

    n_col = 2
    col_w = d_model // n_col
    sub_w = col_w // 2

    def blk(m, t, chip, col, width, core=None):
        row = pl.multiple_of((c if core is None else core) * par_rows + chip * tok, tok)
        return bufs[t][1].at[m, pl.ds(row, tok), pl.ds(col, width)]

    def send(ref, dev, ssem, rsem):
        pltpu.make_async_remote_copy(src_ref=ref, dst_ref=ref, send_sem=ssem, recv_sem=rsem,
                                     device_id=to(dev), device_id_type=MESH).start()

    def ag_start(m):
        for t in range(2):
            own[m * 2 + t].wait()
        for t in range(2):
            for j in range(n_col):
                ref = blk(m, t, z, j * col_w, col_w)
                send(ref, right, ag_send.at[m, t, j], ag_recv.at[m, t, j, 0, 0])
                send(ref, left, ag_send.at[m, t, j], ag_recv.at[m, t, j, 0, 1])
                send(ref, peer, d2d_send.at[m, t, j], d2d_recv.at[m, t, j])

    def ag_event(m, t, j, d):
        last = d == half
        for side in range(2):
            chip = lax.rem(z + (n_chip - d if side == 0 else d), n_chip)
            col, width = (j * col_w, col_w) if not last else (j * col_w + side * sub_w, sub_w)
            ref = blk(m, t, chip, col, width)
            pltpu.make_async_copy(ref, ref, ag_recv.at[m, t, j, d - 1, side]).wait()
            if d < half - 1:
                fwd = ref
            elif d == half - 1:
                fwd = blk(m, t, chip, j * col_w + side * sub_w, sub_w)
            else:
                fwd = None
            if fwd is not None:
                send(fwd, right if side == 0 else left, ag_send.at[m, t, j], ag_recv.at[m, t, j, d, side])
            send(ref, peer, d2d_send.at[m, t, j], d2d_recv.at[m, t, j])

    def peer_blocks(m, t, j, core):
        row = pl.multiple_of(core * par_rows, par_rows)
        return bufs[t][1].at[m, pl.ds(row, par_rows), pl.ds(j * col_w, col_w)]

    def d2d_wait(m, t, j):
        ref = peer_blocks(m, t, j, 1 - c)
        pltpu.make_async_copy(ref, ref, d2d_recv.at[m, t, j]).wait()

    un_rows = unpacked.shape[0]

    def prep_wq():
        wq_cp.wait()
        per = un_rows // heads

        def body(i, _):
            unpacked[...] = stage_q[pl.ds(pl.multiple_of(i * un_rows, un_rows), un_rows), :].astype(F32)
            for h in range(heads):
                wq[pl.ds(pl.multiple_of(i * per, per), per), h * head_dim:(h + 1) * head_dim] = (
                    unpacked[pl.ds(h, per, stride=heads), :].astype(BF16))
            return 0

        lax.fori_loop(0, stage_q.shape[0] // un_rows, body, 0)

    kv_col = pl.multiple_of(c * head_dim, head_dim)

    def prep_kv(i):
        pltpu.make_async_copy(wk_in.at[pl.ds(i * kv_rows, kv_rows)], stage_kv.at[i % 2], kvw_sem.at[i % 2]).wait()
        per = un_rows // kv_heads
        base = i * (kv_rows // kv_heads)

        def body(k, _):
            unpacked[...] = stage_kv[i % 2, pl.ds(pl.multiple_of(k * un_rows, un_rows), un_rows), :].astype(F32)
            wkv[pl.ds(pl.multiple_of(base + k * per, per), per), pl.ds(kv_col, head_dim)] = (
                unpacked[pl.ds(z, per, stride=kv_heads), :].astype(BF16))
            return 0

        lax.fori_loop(0, kv_rows // un_rows, body, 0)
        if i + 2 < n_kv:
            kv_load(i + 2)

    def kv_swap():
        ref = wkv.at[:, pl.ds(kv_col, head_dim)]
        pltpu.make_async_remote_copy(src_ref=ref, dst_ref=ref, send_sem=wx_sem.at[0], recv_sem=wx_sem.at[1],
                                     device_id=to(peer), device_id_type=MESH).start()

    def kv_swap_wait():
        ref = wkv.at[:, pl.ds(kv_col, head_dim)]
        pltpu.make_async_copy(ref, ref, wx_sem.at[0]).wait()
        ref = wkv.at[:, pl.ds(pl.multiple_of((1 - c) * head_dim, head_dim), head_dim)]
        pltpu.make_async_copy(ref, ref, wx_sem.at[1]).wait()

    def proj_x(m, j):
        for k in range(2):
            cols = slice(j * col_w + k * sub_w, j * col_w + (k + 1) * sub_w)
            a = dot(xb[m, :, cols], wq[cols, :])
            b = dot(xb[m, :, cols], wkv[cols, :])
            if j == 0 and k == 0:
                acc_q[...] = a
                acc_kv[...] = b
            else:
                acc_q[...] += a
                acc_kv[...] += b

    def proj_dy(m, j):
        for k in range(2):
            cols = slice(j * col_w + k * sub_w, j * col_w + (k + 1) * sub_w)
            a = dot(dyb[m, :, cols], wo[:, cols], NT)
            if j == 0 and k == 0:
                acc_do[...] = a
            else:
                acc_do[...] += a

    def round_x():
        qb[...] = acc_q[...].astype(BF16)
        kvb[...] = acc_kv[...].astype(BF16)

    def round_dy():
        dob[...] = acc_do[...].astype(BF16)

    def position(axis):
        r = lax.broadcasted_iota(jnp.int32, (n_rows, 1) if axis == 0 else (1, n_rows), axis)
        inner = r % par_rows
        return (inner // tok) * (2 * tok) + (r // par_rows) * tok + inner % tok

    def head(m, h):
        cols = slice(h * head_dim, (h + 1) * head_dim)
        q, k, v = qb[:, cols], kvb[:, :head_dim], kvb[:, head_dim:]
        do = dob[:, cols]
        s = dot(q, k, NT) * scale
        s = jnp.where(position(0) >= position(1), s, -jnp.inf)
        e = jnp.exp(s - jnp.max(s, axis=-1, keepdims=True))
        p = e / jnp.sum(e, axis=-1, keepdims=True)
        pb = p.astype(BF16)
        o = dot(pb, v).astype(BF16)
        ob[m, :, cols] = o
        dp = dot(do, v, NT)
        delta = jnp.sum(do.astype(F32) * o.astype(F32), axis=-1, keepdims=True)
        ds = (p * (dp - delta)).astype(BF16)
        prob_b[h] = pb
        ds_b[h] = ds
        dqb[m, :, cols] = (dot(ds, k) * scale).astype(BF16)

    def head_kv(m, h):
        cols = slice(h * head_dim, (h + 1) * head_dim)
        dk = dot(ds_b[h], qb[:, cols], TN) * scale
        dv = dot(prob_b[h], dob[:, cols], TN)
        if h == 0:
            dkv_f[m, :, :head_dim] = dk
            dkv_f[m, :, head_dim:] = dv
        else:
            dkv_f[m, :, :head_dim] += dk
            dkv_f[m, :, head_dim:] += dv

    def kv_round(m):
        dkvp[...] = dkv_f[m].astype(BF16)
        pltpu.make_async_remote_copy(src_ref=dkv_f.at[m], dst_ref=dkv_peer.at[m], send_sem=dkv_sem.at[m, 0],
                                     recv_sem=dkv_sem.at[m, 1], device_id=to(peer), device_id_type=MESH).start()

    def kv_total(m):
        pltpu.make_async_copy(dkv_f.at[m], dkv_f.at[m], dkv_sem.at[m, 0]).wait()
        pltpu.make_async_copy(dkv_peer.at[m], dkv_peer.at[m], dkv_sem.at[m, 1]).wait()
        dkv_tot[m] = (dkv_f[m] + dkv_peer[m]).astype(BF16)

    rs_n = 4
    rs_w = d_model // rs_n
    rs_h = rs_w // 2

    def dx_chunk(m, j):
        cols = slice(j * rs_w, (j + 1) * rs_w)
        dx_tmp[...] = dot(dqb[m], wq[cols, :], NT) + dot(dkvp[...], wkv[cols, :], NT)
        away = pl.ds(pl.multiple_of((1 - c) * par_rows, par_rows), par_rows)
        keep = pl.ds(pl.multiple_of(c * par_rows, par_rows), par_rows)
        psend[m, :, cols] = dx_tmp[away, :].astype(BF16)
        dx_f[m, :, cols] = dx_tmp[keep, :]
        pltpu.make_async_remote_copy(src_ref=psend.at[m, :, cols], dst_ref=precv.at[m, :, cols],
                                     send_sem=ps_send.at[m, j], recv_sem=ps_recv.at[m, j],
                                     device_id=to(peer), device_id_type=MESH).start()

    def own_part(m, chip, col, width):
        rows = pl.ds(pl.multiple_of(chip * tok, tok), tok)
        return dx_f[m, rows, col:col + width] + precv[m, rows, col:col + width].astype(F32)

    def rs_send_to(m, j, side, d, col, width):
        src = sbuf.at[m, side, d - 1, :, pl.ds(col, width)]
        dst = rbuf.at[m, side, d - 1, :, pl.ds(col, width)]
        pltpu.make_async_remote_copy(src_ref=src, dst_ref=dst, send_sem=rs_send.at[m, j],
                                     recv_sem=rs_recv.at[m, j, d - 1, side],
                                     device_id=to(right if side == 0 else left), device_id_type=MESH).start()

    def chip_at(side, d):
        return lax.rem(z + (d if side == 0 else n_chip - d), n_chip)

    def rs_start(m, j):
        ref = precv.at[m, :, pl.ds(j * rs_w, rs_w)]
        pltpu.make_async_copy(ref, ref, ps_recv.at[m, j]).wait()
        for side in range(2):
            col = j * rs_w + side * rs_h
            sbuf[m, side, half - 1, :, col:col + rs_h] = own_part(m, chip_at(side, half), col, rs_h).astype(BF16)
        for side in range(2):
            rs_send_to(m, j, side, half, j * rs_w + side * rs_h, rs_h)

    def rs_event(m, j, d):
        col = j * rs_w
        for side in range(2):
            rcol, rwidth = (col + side * rs_h, rs_h) if d == half else (col, rs_w)
            ref = rbuf.at[m, side, d - 1, :, pl.ds(rcol, rwidth)]
            pltpu.make_async_copy(ref, ref, rs_recv.at[m, j, d - 1, side]).wait()
        if d == 1:
            total = own_part(m, z, col, rs_w)
            for side in range(2):
                total = total + rbuf[m, side, 0, :, col:col + rs_w].astype(F32)
            dx_own[m, :, col:col + rs_w] = total.astype(BF16)
            return
        for side in range(2):
            chip = chip_at(side, d - 1)
            if d == half:
                a, b = col + side * rs_h, col + (1 - side) * rs_h
                sbuf[m, side, d - 2, :, a:a + rs_h] = (
                    own_part(m, chip, a, rs_h) + rbuf[m, side, d - 1, :, a:a + rs_h].astype(F32)).astype(BF16)
                sbuf[m, side, d - 2, :, b:b + rs_h] = own_part(m, chip, b, rs_h).astype(BF16)
            else:
                sbuf[m, side, d - 2, :, col:col + rs_w] = (
                    own_part(m, chip, col, rs_w)
                    + rbuf[m, side, d - 1, :, col:col + rs_w].astype(F32)).astype(BF16)
        for side in range(2):
            rs_send_to(m, j, side, d - 1, col, rs_w)

    outs = []

    def write_out(src, dst):
        cp = pltpu.make_async_copy(src, dst, out_sem.at[len(outs)])
        cp.start()
        outs.append(cp)

    tensor_cols = [(t, j) for t in range(2) for j in range(n_col)]

    ag_start(0)
    work = [prep_wq] + [functools.partial(prep_kv, i) for i in range(n_kv)] + [kv_swap]
    slots = [(d, t, j) for d in range(1, half) for t, j in tensor_cols]
    for s, (d, t, j) in enumerate(slots):
        ag_event(0, t, j, d)
        if work:
            work.pop(0)()
    for w in work:
        w()
    ag_start(1)
    wo_cp.wait()
    kv_swap_wait()

    def finish_gather(m, extra):
        for t, j in tensor_cols:
            ag_event(m, t, j, half)
            for f in extra.get((t, j), ()):
                f()
            if (t, j) == (0, 0):
                continue
            pt, pj = tensor_cols[tensor_cols.index((t, j)) - 1]
            finish_part(m, pt, pj)
        finish_part(m, *tensor_cols[-1])
        write_out(xb.at[m], xf_out.at[m])
        write_out(dyb.at[m], dyf_out.at[m])

    def finish_part(m, t, j):
        d2d_wait(m, t, j)
        (proj_x if t == 0 else proj_dy)(m, j)
        if j == n_col - 1:
            (round_x if t == 0 else round_dy)()

    def attn_steps(m):
        steps = []
        for h in range(heads):
            steps.append(functools.partial(head, m, h))
            steps.append(functools.partial(head_kv, m, h))
        steps.append(functools.partial(kv_round, m))
        return steps

    finish_gather(0, {})
    work = attn_steps(0) + [functools.partial(dx_chunk, 0, j) for j in range(rs_n)] + [functools.partial(kv_total, 0)]
    for s, (d, t, j) in enumerate(slots):
        ag_event(1, t, j, d)
        if work:
            work.pop(0)()
    for w in work:
        w()
    for j in range(rs_n):
        rs_start(0, j)
    finish_gather(1, {})
    work = attn_steps(1) + [functools.partial(dx_chunk, 1, j) for j in range(rs_n)]
    for d in range(half, 1, -1):
        for j in range(rs_n):
            rs_event(0, j, d)
            if work:
                work.pop(0)()
    for w in work:
        w()
    for j in range(rs_n):
        rs_event(0, j, 1)
        rs_start(1, j)
    write_out(dx_own.at[0], dx_out.at[0])
    kv_total(1)
    for m in range(micro_n):
        write_out(dqb.at[m], dq_out.at[m])
        write_out(dkv_tot.at[m], dkv_out.at[m])
        write_out(ob.at[m], o_out.at[m])
    for d in range(half, 0, -1):
        for j in range(rs_n):
            rs_event(1, j, d)
    write_out(dx_own.at[1], dx_out.at[1])

    for m in range(micro_n):
        for t, j in tensor_cols:
            rows = n_chip - 1
            ref = bufs[t][1].at[m, pl.ds(0, rows * tok), pl.ds(j * col_w, col_w)]
            pltpu.make_async_copy(ref, ref, ag_send.at[m, t, j]).wait()
            ref = peer_blocks(m, t, j, c)
            pltpu.make_async_copy(ref, ref, d2d_send.at[m, t, j]).wait()
        for j in range(rs_n):
            ref = psend.at[m, :, pl.ds(j * rs_w, rs_w)]
            pltpu.make_async_copy(ref, ref, ps_send.at[m, j]).wait()
            ref = psend.at[m, pl.ds(0, (n_chip - 1) * tok), pl.ds(j * rs_w, rs_w)]
            pltpu.make_async_copy(ref, ref, rs_send.at[m, j]).wait()
    for cp in outs:
        cp.wait()


def grad_kernel(heads, col_half, xf, xh, dyf, dq, dkv, o, dwq, dwk, dwv, dwo, tmp):
    micro_n = xf.shape[0]
    head_dim = dkv.shape[2] // 2
    tile = xf.shape[2]
    acc = sum(dot(xf[m], dq[m], TN) for m in range(micro_n))
    for h in range(heads):
        dwq[pl.ds(h, tile, stride=heads), :] = acc[:, h * head_dim:(h + 1) * head_dim]
    acc = sum(dot(xh[m], dkv[m], TN) for m in range(micro_n))
    dwk[...] = acc[:, :head_dim]
    dwv[...] = acc[:, head_dim:]
    dwo[...] = sum(dot(o[m], dyf[m], TN) for m in range(micro_n))


def solution(mesh):
    n_dev = mesh.shape["model"]

    def device_grads(x_loc, dy_loc, w_q, w_k, w_v, w_o):
        micro_n, tok, d_model = x_loc.shape
        heads, head_dim = w_q.shape[1], w_q.shape[2]
        kv_heads = w_k.shape[1]
        n_rows = tok * n_dev
        par_rows = n_rows // 2
        hd = heads * head_dim
        n_chip = n_dev // 2
        half = n_chip // 2
        any_spec = pl.BlockSpec(memory_space=pl.ANY)
        dma = pltpu.SemaphoreType.DMA
        scratch = [
            pltpu.VMEM((micro_n, n_rows, d_model), BF16),
            pltpu.VMEM((micro_n, n_rows, d_model), BF16),
            pltpu.VMEM((d_model, hd), BF16),
            pltpu.VMEM((hd, d_model), BF16),
            pltpu.VMEM((d_model, 2 * head_dim), BF16),
            pltpu.VMEM((d_model * heads, head_dim), BF16),
            pltpu.VMEM((2, d_model * kv_heads // 8, head_dim), BF16),
            pltpu.VMEM((512, head_dim), F32),
            pltpu.VMEM((n_rows, hd), F32),
            pltpu.VMEM((n_rows, 2 * head_dim), F32),
            pltpu.VMEM((n_rows, hd), F32),
            pltpu.VMEM((n_rows, hd), BF16),
            pltpu.VMEM((n_rows, 2 * head_dim), BF16),
            pltpu.VMEM((n_rows, hd), BF16),
            pltpu.VMEM((micro_n, n_rows, hd), BF16),
            pltpu.VMEM((micro_n, n_rows, hd), BF16),
            pltpu.VMEM((n_rows, 2 * head_dim), BF16),
            pltpu.VMEM((heads, n_rows, n_rows), BF16),
            pltpu.VMEM((heads, n_rows, n_rows), BF16),
            pltpu.VMEM((micro_n, n_rows, 2 * head_dim), F32),
            pltpu.VMEM((micro_n, n_rows, 2 * head_dim), F32),
            pltpu.VMEM((micro_n, n_rows, 2 * head_dim), BF16),
            pltpu.VMEM((micro_n, par_rows, d_model), F32),
            pltpu.VMEM((n_rows, d_model // 4), F32),
            pltpu.VMEM((micro_n, par_rows, d_model), BF16),
            pltpu.VMEM((micro_n, par_rows, d_model), BF16),
            pltpu.VMEM((micro_n, 2, half, tok, d_model), BF16),
            pltpu.VMEM((micro_n, 2, half, tok, d_model), BF16),
            pltpu.VMEM((micro_n, tok, d_model), BF16),
            dma((micro_n, 2)), dma((2,)), dma((2,)), dma((6 * micro_n,)),
            dma((micro_n, 2, 2)), dma((micro_n, 2, 2, half, 2)),
            dma((micro_n, 2, 2)), dma((micro_n, 2, 2)), dma((2,)),
            dma((micro_n, 2)), dma((micro_n, 4)), dma((micro_n, 4)),
            dma((micro_n, 4)), dma((micro_n, 4, half, 2)),
        ]
        dx, xf, dyf, dq, dkv, o = pl.pallas_call(
            functools.partial(attn_kernel, n_dev, kv_heads),
            out_shape=(
                jax.ShapeDtypeStruct((micro_n, tok, d_model), BF16),
                jax.ShapeDtypeStruct((micro_n, n_rows, d_model), BF16),
                jax.ShapeDtypeStruct((micro_n, n_rows, d_model), BF16),
                jax.ShapeDtypeStruct((micro_n, n_rows, hd), BF16),
                jax.ShapeDtypeStruct((micro_n, n_rows, 2 * head_dim), BF16),
                jax.ShapeDtypeStruct((micro_n, n_rows, hd), BF16),
            ),
            in_specs=[any_spec] * 6,
            out_specs=(any_spec,) * 6,
            scratch_shapes=scratch,
            compiler_params=pltpu.CompilerParams(collective_id=0, has_side_effects=True,
                                                 vmem_limit_bytes=60 * 1024 * 1024),
        )(x_loc, dy_loc, w_q.reshape(d_model * heads, head_dim), w_k.reshape(d_model * kv_heads, head_dim),
          w_v.reshape(d_model * kv_heads, head_dim), w_o.reshape(hd, d_model))

        core = (lax.axis_index("model") % 2).astype(jnp.int32).reshape(1)
        steps = 10
        tile = d_model // steps
        half_tile = tile // 2
        full = lambda i, s: (0, 0, 0)
        dwq, dwk, dwv, dwo = pl.pallas_call(
            lambda s, *refs: grad_kernel(heads, half_tile, *refs, None),
            grid_spec=pltpu.PrefetchScalarGridSpec(
                num_scalar_prefetch=1,
                grid=(steps,),
                in_specs=[
                    pl.BlockSpec((micro_n, n_rows, tile), lambda i, s: (0, 0, i)),
                    pl.BlockSpec((micro_n, n_rows, half_tile), lambda i, s: (0, 0, s[0] * steps + i)),
                    pl.BlockSpec((micro_n, n_rows, tile), lambda i, s: (0, 0, i)),
                    pl.BlockSpec((micro_n, n_rows, hd), full),
                    pl.BlockSpec((micro_n, n_rows, 2 * head_dim), full),
                    pl.BlockSpec((micro_n, n_rows, hd), full),
                ],
                out_specs=[
                    pl.BlockSpec((tile * heads, head_dim), lambda i, s: (i, 0)),
                    pl.BlockSpec((half_tile, head_dim), lambda i, s: (i, 0)),
                    pl.BlockSpec((half_tile, head_dim), lambda i, s: (i, 0)),
                    pl.BlockSpec((hd, tile), lambda i, s: (0, i)),
                ],
            ),
            out_shape=(
                jax.ShapeDtypeStruct((d_model * heads, head_dim), F32),
                jax.ShapeDtypeStruct((d_model // 2, head_dim), F32),
                jax.ShapeDtypeStruct((d_model // 2, head_dim), F32),
                jax.ShapeDtypeStruct((hd, d_model), F32),
            ),
        )(core, xf, xf, dyf, dq, dkv, o)
        return dx, dwq.reshape(d_model, heads, head_dim), dwk, dwv, dwo.reshape(heads, head_dim, d_model)

    return jax.shard_map(
        device_grads, mesh=mesh,
        in_specs=(P("data", "model", None), P("data", "model", None), P(None, "model", None),
                  P(None, None, None), P(None, None, None), P("model", None, None)),
        out_specs=(P("data", "model", None), P("data", "model", None), P(("data", "model"), None),
                   P(("data", "model"), None), P(("data", "model"), None, None)),
        check_vma=False)
```

time: 297 us -> 111 us (0.37)
  waiting for transfers between devices: 175 us -> 0 us
  Pallas kernels: 0 us -> 109 us
  matrix products: 53.2 us -> 0 us
  local copies, waits for them, and re-layouts: 39.9 us -> 0.73 us
  between operations: 14.6 us -> 0.66 us
  other arithmetic: 12.5 us -> 0 us
    pallas_call x0 -> x2, Pallas kernels: none -> 109 us  [the longest x1 94.3 us: device_grads(): pl.pallas_call(functools.partial(attn_kernel, n_dev, kv_heads), out_shape...]
    all_gather x4 -> x0, waiting for transfers between devices: 106 us -> none  [the longest x2 65.1 us: device_grads(): x_full = lax.all_gather(x_loc[micro_idx], 'model', axis=0, tiled=True)]
    reduce_scatter x2 -> x0, waiting for transfers between devices: 67.5 us -> none  [device_grads(): dx_own = lax.psum_scatter(dx_part, 'model', scatter_dimension=0, tiled=True)]
    dot_general x32 -> x0, matrix products: 49.9 us -> none  [the longest x2 8.18 us: device_grads(): jnp.einsum('sc,hec->she', dy_full, w_o, preferred_element_type=jnp.float32)]
    unnamed x57 -> x3, local copies, waits for them, and re-layouts: 23.3 us -> 0.73 us
    dynamic_slice x2 -> x0, local copies, waits for them, and re-layouts: 13 us -> none  [the longest x1 6.51 us: device_grads(): w_k_own = lax.dynamic_index_in_dim(w_k, kv_index, axis=1, keepdims=False)]
    add x2 -> x0, other arithmetic: 6.08 us -> none  [sub_reduce_scatter(): part_sum = kept_half + lax.ppermute(sent_half, 'model', pair_list)]
    slice x2 -> x0, local copies, waits for them, and re-layouts: 3.62 us -> none  [the longest x1 1.89 us: device_grads(): dy_full = lax.all_gather(dy_loc[micro_idx], 'model', axis=0, tiled=True)]
  transfers between devices with their start and end apart: 8 -> 0, of which waited for: 6 -> 0; matrix products, arithmetic and copies ran while one was open for 33% -> 0% of each run, Pallas kernels for 0% -> 0%
where the time goes in v1:
time: 111 us; the launch traced here: 110 us
  Pallas kernels  109 us (98%)
    pallas_call x1, Pallas kernels, device_grads(): pl.pallas_call(functools.partial(attn_kernel, n_dev, kv_heads), out_shape...  94.3 us
    pallas_call x1, Pallas kernels, device_grads(): pl.pallas_call(lambda s, *refs: grad_kernel(heads, half_tile, *refs, None...  14.6 us

profile of v1, /device:TPU:22, one launch (start us, length us, event | category | flops | bytes accessed | tf_op | source)
XLA Modules:
  0.0 110.2 jit_solution(7251721908593761748)
XLA Ops:
  0.6 94.3 %shard_map.101 = (bf16[2,16,5120]{2,1,0:T(8,128)(2,1)}, bf16[2,256,5120]{2,1,0:T(8,128)(2,1)}, bf16[2,256,5120]{2,1,0:T(8,128)(2,1)}, bf16[2,256,256]{2,1,0:T(8,...) custom-call(bf16[2,16,5120]{2,1,0:T(8,128)(2,1)} %x_in.1, bf16[2,16,5120]{2,1,0:T(8,128)(2,1)} %dy_in.1, ...), custom_call_target="tpu_custom_call" | custom-call | tf_op jit(solution)/shard_map/pallas_call | solution.py:468
  94.9 0.0 copy-start
  94.9 14.6 %shard_map.102 = (f32[10240,128]{1,0:T(8,128)}, f32[2560,128]{1,0:T(8,128)}, f32[2560,128]{1,0:T(8,128)}, f32[256,5120]{1,0:T(8,128)}) custom-call(s32[1]{0:T(128)} %bitcast.4.s, bf16[2,256,5120]{2,1,0:T(8,128)(2,1)} %get-tuple-element.16.refs_0_.refs_1_, bf16[2,256,5120]{2,1,0:T(8,128)(2,1)} %get-tuple-element.16.refs_0_.refs_1_, ...), custom_call_target="tpu_custom_call" | custom-call | tf_op jit(solution)/shard_map/pallas_call | solution.py:491
  109.5 0.0 copy-done
  109.5 0.7 copy.12
Async XLA Ops:
  94.9 14.6 %copy-start = (bf16[2,16,5120]{2,1,0:T(8,128)(2,1)S(1)}, bf16[2,16,5120]{2,1,0:T(8,128)(2,1)}, u32[]{:S(2)}) copy-start(bf16[2,16,5120]{2,1,0:T(8,128)(2,1)} %get-tuple-element.30) | copy-start | bytes 983044

commit v2 on v1

--- a/solution.py
+++ b/solution.py
@@ -21,7 +21,7 @@
 
 
 def attn_kernel(n_dev, kv_heads, x_in, dy_in, wq_in, wk_in, wv_in, wo_in,
-                dx_out, xf_out, dyf_out, dq_out, dkv_out, o_out,
+                dx_out, dwq, dwk, dwv, dwo,
                 xb, dyb, wq, wo, wkv, stage_q, stage_kv, unpacked,
                 acc_q, acc_kv, acc_do, qb, kvb, dob, ob, dqb, dkvp, prob_b, ds_b,
                 dkv_f, dkv_peer, dkv_tot,
@@ -239,6 +239,37 @@
         pltpu.make_async_copy(dkv_f.at[m], dkv_f.at[m], dkv_sem.at[m, 0]).wait()
         pltpu.make_async_copy(dkv_peer.at[m], dkv_peer.at[m], dkv_sem.at[m, 1]).wait()
         dkv_tot[m] = (dkv_f[m] + dkv_peer[m]).astype(BF16)
+
+    dw_n = 4
+    dw_w = d_model // dw_n
+
+    def put(ref, idx, val, m):
+        if m == 0:
+            ref[idx] = val
+        else:
+            ref[idx] += val
+
+    def dw_x(m, i):
+        ck = lax.rem(c * (dw_n // 2) + i, dw_n)
+        start = pl.multiple_of(ck * dw_w, dw_w)
+        xt = xb[m, :, pl.ds(start, dw_w)].T
+        g = dot(xt, dqb[m])
+        for h in range(heads):
+            put(dwq, (pl.ds(start * heads + h, dw_w, stride=heads), slice(None)),
+                g[:, h * head_dim:(h + 1) * head_dim], m)
+        if i < dw_n // 2:
+            g = dot(xt, dkv_tot[m])
+            rows = slice(i * dw_w, (i + 1) * dw_w)
+            put(dwk, (rows, slice(None)), g[:, :head_dim], m)
+            put(dwv, (rows, slice(None)), g[:, head_dim:], m)
+
+    def dw_o(m, i):
+        cols = slice(i * dw_w, (i + 1) * dw_w)
+        put(dwo, (slice(None), cols), dot(ob[m], dyb[m, :, cols], TN), m)
+
+    def dw_steps(m):
+        return ([functools.partial(dw_o, m, i) for i in range(dw_n)]
+                + [functools.partial(dw_x, m, i) for i in range(dw_n)])
 
     rs_n = 4
     rs_w = d_model // rs_n
@@ -336,8 +367,6 @@
             pt, pj = tensor_cols[tensor_cols.index((t, j)) - 1]
             finish_part(m, pt, pj)
         finish_part(m, *tensor_cols[-1])
-        write_out(xb.at[m], xf_out.at[m])
-        write_out(dyb.at[m], dyf_out.at[m])
 
     def finish_part(m, t, j):
         d2d_wait(m, t, j)
@@ -354,13 +383,11 @@
         return steps
 
     finish_gather(0, {})
-    work = attn_steps(0) + [functools.partial(dx_chunk, 0, j) for j in range(rs_n)] + [functools.partial(kv_total, 0)]
-    for s, (d, t, j) in enumerate(slots):
+    work = attn_steps(0) + [functools.partial(dx_chunk, 0, j) for j in range(rs_n)]
+    later = [functools.partial(kv_total, 0)] + dw_steps(0)
+    for d, t, j in slots:
         ag_event(1, t, j, d)
-        if work:
-            work.pop(0)()
-    for w in work:
-        w()
+        (work or later).pop(0)()
     for j in range(rs_n):
         rs_start(0, j)
     finish_gather(1, {})
@@ -368,22 +395,19 @@
     for d in range(half, 1, -1):
         for j in range(rs_n):
             rs_event(0, j, d)
-            if work:
-                work.pop(0)()
-    for w in work:
-        w()
+            (work or later).pop(0)()
+    for j in range(rs_n):
+        rs_start(1, j)
+    later += [functools.partial(kv_total, 1)] + dw_steps(1)
     for j in range(rs_n):
         rs_event(0, j, 1)
-        rs_start(1, j)
+        later.pop(0)()
     write_out(dx_own.at[0], dx_out.at[0])
-    kv_total(1)
-    for m in range(micro_n):
-        write_out(dqb.at[m], dq_out.at[m])
-        write_out(dkv_tot.at[m], dkv_out.at[m])
-        write_out(ob.at[m], o_out.at[m])
     for d in range(half, 0, -1):
         for j in range(rs_n):
             rs_event(1, j, d)
+            if later:
+                later.pop(0)()
     write_out(dx_own.at[1], dx_out.at[1])
 
     for m in range(micro_n):
@@ -400,19 +424,6 @@
             pltpu.make_async_copy(ref, ref, rs_send.at[m, j]).wait()
     for cp in outs:
         cp.wait()
-
-
-def grad_kernel(heads, col_half, xf, xh, dyf, dq, dkv, o, dwq, dwk, dwv, dwo, tmp):
-    micro_n = xf.shape[0]
-    head_dim = dkv.shape[2] // 2
-    tile = xf.shape[2]
-    acc = sum(dot(xf[m], dq[m], TN) for m in range(micro_n))
-    for h in range(heads):
-        dwq[pl.ds(h, tile, stride=heads), :] = acc[:, h * head_dim:(h + 1) * head_dim]
-    acc = sum(dot(xh[m], dkv[m], TN) for m in range(micro_n))
-    dwk[...] = acc[:, :head_dim]
-    dwv[...] = acc[:, head_dim:]
-    dwo[...] = sum(dot(o[m], dyf[m], TN) for m in range(micro_n))
 
 
 def solution(mesh):
@@ -465,56 +476,23 @@
             dma((micro_n, 2)), dma((micro_n, 4)), dma((micro_n, 4)),
             dma((micro_n, 4)), dma((micro_n, 4, half, 2)),
         ]
-        dx, xf, dyf, dq, dkv, o = pl.pallas_call(
+        dx, dwq, dwk, dwv, dwo = pl.pallas_call(
             functools.partial(attn_kernel, n_dev, kv_heads),
             out_shape=(
                 jax.ShapeDtypeStruct((micro_n, tok, d_model), BF16),
-                jax.ShapeDtypeStruct((micro_n, n_rows, d_model), BF16),
-                jax.ShapeDtypeStruct((micro_n, n_rows, d_model), BF16),
-                jax.ShapeDtypeStruct((micro_n, n_rows, hd), BF16),
-                jax.ShapeDtypeStruct((micro_n, n_rows, 2 * head_dim), BF16),
-                jax.ShapeDtypeStruct((micro_n, n_rows, hd), BF16),
+                pltpu.VMEM((d_model * heads, head_dim), F32),
+                pltpu.VMEM((d_model // 2, head_dim), F32),
+                pltpu.VMEM((d_model // 2, head_dim), F32),
+                pltpu.VMEM((hd, d_model), F32),
             ),
             in_specs=[any_spec] * 6,
-            out_specs=(any_spec,) * 6,
+            out_specs=(any_spec,) + (pl.BlockSpec(memory_space=pltpu.VMEM),) * 4,
             scratch_shapes=scratch,
             compiler_params=pltpu.CompilerParams(collective_id=0, has_side_effects=True,
-                                                 vmem_limit_bytes=60 * 1024 * 1024),
+                                                 vmem_limit_bytes=46 * 1024 * 1024),
         )(x_loc, dy_loc, w_q.reshape(d_model * heads, head_dim), w_k.reshape(d_model * kv_heads, head_dim),
           w_v.reshape(d_model * kv_heads, head_dim), w_o.reshape(hd, d_model))
 
-        core = (lax.axis_index("model") % 2).astype(jnp.int32).reshape(1)
-        steps = 10
-        tile = d_model // steps
-        half_tile = tile // 2
-        full = lambda i, s: (0, 0, 0)
-        dwq, dwk, dwv, dwo = pl.pallas_call(
-            lambda s, *refs: grad_kernel(heads, half_tile, *refs, None),
-            grid_spec=pltpu.PrefetchScalarGridSpec(
-                num_scalar_prefetch=1,
-                grid=(steps,),
-                in_specs=[
-                    pl.BlockSpec((micro_n, n_rows, tile), lambda i, s: (0, 0, i)),
-                    pl.BlockSpec((micro_n, n_rows, half_tile), lambda i, s: (0, 0, s[0] * steps + i)),
-                    pl.BlockSpec((micro_n, n_rows, tile), lambda i, s: (0, 0, i)),
-                    pl.BlockSpec((micro_n, n_rows, hd), full),
-                    pl.BlockSpec((micro_n, n_rows, 2 * head_dim), full),
-                    pl.BlockSpec((micro_n, n_rows, hd), full),
-                ],
-                out_specs=[
-                    pl.BlockSpec((tile * heads, head_dim), lambda i, s: (i, 0)),
-                    pl.BlockSpec((half_tile, head_dim), lambda i, s: (i, 0)),
-                    pl.BlockSpec((half_tile, head_dim), lambda i, s: (i, 0)),
-                    pl.BlockSpec((hd, tile), lambda i, s: (0, i)),
-                ],
-            ),
-            out_shape=(
-                jax.ShapeDtypeStruct((d_model * heads, head_dim), F32),
-                jax.ShapeDtypeStruct((d_model // 2, head_dim), F32),
-                jax.ShapeDtypeStruct((d_model // 2, head_dim), F32),
-                jax.ShapeDtypeStruct((hd, d_model), F32),
-            ),
-        )(core, xf, xf, dyf, dq, dkv, o)
         return dx, dwq.reshape(d_model, heads, head_dim), dwk, dwv, dwo.reshape(heads, head_dim, d_model)
 
     return jax.shard_map(

time: 111 us -> 102 us (0.919)
  Pallas kernels: 109 us -> 93.4 us
  local copies, waits for them, and re-layouts: 0.73 us -> 7.56 us
    pallas_call x1 -> x0, Pallas kernels: 14.6 us -> none  [device_grads(): pl.pallas_call(lambda s, *refs: grad_kernel(heads, half_tile, *refs, None...]
    unnamed x3 -> x7, local copies, waits for them, and re-layouts: 0.73 us -> 7.56 us
where the time goes in v2:
time: 102 us
  Pallas kernels  93.4 us (92%)
  local copies, waits for them, and re-layouts  7.56 us (7%)
    pallas_call x1, Pallas kernels, device_grads(): pl.pallas_call(functools.partial(attn_kernel, n_dev, kv_heads), out_shape...  93.4 us
    unnamed x7, local copies, waits for them, and re-layouts  7.56 us

profile of v2, /device:TPU:22, one launch (start us, length us, event | category | flops | bytes accessed | tf_op | source)
XLA Modules:
  0.0 101.6 jit_solution(1886204774492047211)
XLA Ops:
  0.6 93.4 %shard_map.101 = (bf16[2,16,5120]{2,1,0:T(8,128)(2,1)}, f32[10240,128]{1,0:T(8,128)S(1)}, f32[2560,128]{1,0:T(8,128)S(1)}, f32[2560,128]{1,0:T(8,128)S(1)}, f32[256,5120]{1,0:T(8,128)S(1)}) custom-call(bf16[2,16,5120]{2,1,0:T(8,128)(2,1)} %x_in.1, bf16[2,16,5120]{2,1,0:T(8,128)(2,1)} %dy_in.1, bf16[10240,128]{1,0:T(8,128)(2,1)} %bitcast.10, ...), custom_call_target="tpu_custom_call" | custom-call | tf_op jit(solution)/shard_map/pallas_call | solution.py:479
  94.0 2.4 %copy.16 = f32[5120,2,128]{2,1,0:T(2,128)} copy(f32[5120,2,128]{2,1,0:T(2,128)S(1)} %bitcast.7) | data formatting | bytes 10485760
  96.4 1.1 %copy.17 = f32[2560,128]{1,0:T(8,128)} copy(f32[2560,128]{1,0:T(8,128)S(1)} %get-tuple-element.17) | data formatting | bytes 2621440
  97.4 1.1 %copy.18 = f32[2560,128]{1,0:T(8,128)} copy(f32[2560,128]{1,0:T(8,128)S(1)} %get-tuple-element.18) | data formatting | bytes 2621440
  98.5 0.0 copy-start
  98.5 2.4 %copy.19 = f32[2,128,5120]{2,1,0:T(8,128)} copy(f32[2,128,5120]{2,1,0:T(8,128)S(1)} %bitcast.6) | data formatting | bytes 10485760
  100.9 0.0 copy-done
  100.9 0.7 copy.20
Async XLA Ops:
  98.5 2.4 %copy-start = (bf16[2,16,5120]{2,1,0:T(8,128)(2,1)S(1)}, bf16[2,16,5120]{2,1,0:T(8,128)(2,1)}, u32[]{:S(2)}) copy-start(bf16[2,16,5120]{2,1,0:T(8,128)(2,1)} %get-tuple-element.25) | copy-start | bytes 983044

commit v3 on v2

--- a/solution.py
+++ b/solution.py
@@ -21,12 +21,12 @@
 
 
 def attn_kernel(n_dev, kv_heads, x_in, dy_in, wq_in, wk_in, wv_in, wo_in,
-                dx_out, dwq, dwk, dwv, dwo,
+                dx_own, dwq, dwk, dwv, dwo,
                 xb, dyb, wq, wo, wkv, stage_q, stage_kv, unpacked,
                 acc_q, acc_kv, acc_do, qb, kvb, dob, ob, dqb, dkvp, prob_b, ds_b,
                 dkv_f, dkv_peer, dkv_tot,
-                dx_f, dx_tmp, psend, precv, sbuf, rbuf, dx_own,
-                own_sem, w_sem, kvw_sem, out_sem,
+                dx_f, dx_tmp, psend, precv, sbuf, rbuf,
+                own_sem, w_sem, kvw_sem,
                 ag_send, ag_recv, d2d_send, d2d_recv, wx_sem,
                 dkv_sem, ps_send, ps_recv, rs_send, rs_recv):
     n_chip = n_dev // 2
@@ -335,13 +335,6 @@
         for side in range(2):
             rs_send_to(m, j, side, d - 1, col, rs_w)
 
-    outs = []
-
-    def write_out(src, dst):
-        cp = pltpu.make_async_copy(src, dst, out_sem.at[len(outs)])
-        cp.start()
-        outs.append(cp)
-
     tensor_cols = [(t, j) for t in range(2) for j in range(n_col)]
 
     ag_start(0)
@@ -402,13 +395,11 @@
     for j in range(rs_n):
         rs_event(0, j, 1)
         later.pop(0)()
-    write_out(dx_own.at[0], dx_out.at[0])
     for d in range(half, 0, -1):
         for j in range(rs_n):
             rs_event(1, j, d)
             if later:
                 later.pop(0)()
-    write_out(dx_own.at[1], dx_out.at[1])
 
     for m in range(micro_n):
         for t, j in tensor_cols:
@@ -422,7 +413,14 @@
             pltpu.make_async_copy(ref, ref, ps_send.at[m, j]).wait()
             ref = psend.at[m, pl.ds(0, (n_chip - 1) * tok), pl.ds(j * rs_w, rs_w)]
             pltpu.make_async_copy(ref, ref, rs_send.at[m, j]).wait()
-    for cp in outs:
+
+
+def copy_kernel(n, *refs):
+    srcs, dsts, sem = refs[:n], refs[n:2 * n], refs[2 * n]
+    copies = [pltpu.make_async_copy(a, b, sem.at[i]) for i, (a, b) in enumerate(zip(srcs, dsts))]
+    for cp in copies:
+        cp.start()
+    for cp in copies:
         cp.wait()
 
 
@@ -469,8 +467,7 @@
             pltpu.VMEM((micro_n, par_rows, d_model), BF16),
             pltpu.VMEM((micro_n, 2, half, tok, d_model), BF16),
             pltpu.VMEM((micro_n, 2, half, tok, d_model), BF16),
-            pltpu.VMEM((micro_n, tok, d_model), BF16),
-            dma((micro_n, 2)), dma((2,)), dma((2,)), dma((6 * micro_n,)),
+            dma((micro_n, 2)), dma((2,)), dma((2,)),
             dma((micro_n, 2, 2)), dma((micro_n, 2, 2, half, 2)),
             dma((micro_n, 2, 2)), dma((micro_n, 2, 2)), dma((2,)),
             dma((micro_n, 2)), dma((micro_n, 4)), dma((micro_n, 4)),
@@ -479,20 +476,29 @@
         dx, dwq, dwk, dwv, dwo = pl.pallas_call(
             functools.partial(attn_kernel, n_dev, kv_heads),
             out_shape=(
-                jax.ShapeDtypeStruct((micro_n, tok, d_model), BF16),
+                pltpu.VMEM((micro_n, tok, d_model), BF16),
                 pltpu.VMEM((d_model * heads, head_dim), F32),
                 pltpu.VMEM((d_model // 2, head_dim), F32),
                 pltpu.VMEM((d_model // 2, head_dim), F32),
                 pltpu.VMEM((hd, d_model), F32),
             ),
             in_specs=[any_spec] * 6,
-            out_specs=(any_spec,) + (pl.BlockSpec(memory_space=pltpu.VMEM),) * 4,
+            out_specs=(pl.BlockSpec(memory_space=pltpu.VMEM),) * 5,
             scratch_shapes=scratch,
             compiler_params=pltpu.CompilerParams(collective_id=0, has_side_effects=True,
                                                  vmem_limit_bytes=46 * 1024 * 1024),
         )(x_loc, dy_loc, w_q.reshape(d_model * heads, head_dim), w_k.reshape(d_model * kv_heads, head_dim),
           w_v.reshape(d_model * kv_heads, head_dim), w_o.reshape(hd, d_model))
 
+        grads = (dx, dwq, dwk, dwv, dwo)
+        dx, dwq, dwk, dwv, dwo = pl.pallas_call(
+            functools.partial(copy_kernel, len(grads)),
+            out_shape=tuple(jax.ShapeDtypeStruct(g.shape, g.dtype) for g in grads),
+            in_specs=[pl.BlockSpec(memory_space=pltpu.VMEM)] * len(grads),
+            out_specs=(any_spec,) * len(grads),
+            scratch_shapes=[dma((len(grads),))],
+            compiler_params=pltpu.CompilerParams(vmem_limit_bytes=1024 * 1024),
+        )(*grads)
         return dx, dwq.reshape(d_model, heads, head_dim), dwk, dwv, dwo.reshape(heads, head_dim, d_model)
 
     return jax.shard_map(

time: 102 us -> 98.6 us (0.967)
  local copies, waits for them, and re-layouts: 7.56 us -> 0 us
  Pallas kernels: 93.4 us -> 97.7 us
    unnamed x7 -> x0, local copies, waits for them, and re-layouts: 7.56 us -> none
    pallas_call x0 -> x1, Pallas kernels: none -> 5.03 us  [device_grads(): pl.pallas_call(functools.partial(copy_kernel, len(grads)), out_shape=tupl...]
where the time goes in v3:
time: 98.6 us; the launch traced here: 98.5 us
  Pallas kernels  97.7 us (99%)
    pallas_call x1, Pallas kernels, device_grads(): pl.pallas_call(functools.partial(attn_kernel, n_dev, kv_heads), out_shape...  92.7 us
    pallas_call x1, Pallas kernels, device_grads(): pl.pallas_call(functools.partial(copy_kernel, len(grads)), out_shape=tupl...  5.03 us

profile of v3, /device:TPU:22, one launch (start us, length us, event | category | flops | bytes accessed | tf_op | source)
XLA Modules:
  0.0 98.5 jit_solution(13508713738902128540)
XLA Ops:
  0.6 92.7 %shard_map.101 = (bf16[2,16,5120]{2,1,0:T(8,128)(2,1)S(1)}, f32[10240,128]{1,0:T(8,128)S(1)}, f32[2560,128]{1,0:T(8,128)S(1)}, f32[2560,128]{1,0:T(8,128)S(1)}, f32[256,5120]{1,0:T(8,128)S(1)}) custom-call(bf16[2,16,5120]{2,1,0:T(8,128)(2,1)} %x_in.1, bf16[2,16,5120]{2,1,0:T(8,128)(2,1)} %dy_in.1, bf16[10240,128]{1,0:T(8,128)(2,1)} %bitcast.8, ...), custom_call_target="tpu_custom_call" | custom-call | tf_op jit(solution)/shard_map/pallas_call | solution.py:476
  93.3 5.0 %shard_map.102 = (bf16[2,16,5120]{2,1,0:T(8,128)(2,1)}, f32[10240,128]{1,0:T(8,128)}, f32[2560,128]{1,0:T(8,128)}, f32[2560,128]{1,0:T(8,128)}, f32[256,5120]{1,0:T(8,128)}) custom-call(bf16[2,16,5120]{2,1,0:T(8,128)(2,1)S(1)} %get-tuple-element.15.refs_0_, f32[10240,128]{1,0:T(8,128)S(1)} %get-tuple-element.16.refs_1_, ...), custom_call_target="tpu_custom_call" | custom-call | tf_op jit(solution)/shard_map/pallas_call | solution.py:494

commit v4 on v3

--- a/solution.py
+++ b/solution.py
@@ -46,6 +46,10 @@
     def to(dev):
         return {"model": dev}
 
+    barrier = pltpu.get_barrier_semaphore()
+    for dev in (left, right, peer):
+        pl.semaphore_signal(barrier, inc=1, device_id=to(dev), device_id_type=MESH)
+
     bufs = ((x_in, xb), (dy_in, dyb))
     my_row = pl.multiple_of(c * par_rows + z * tok, tok)
     own = []
@@ -73,9 +77,6 @@
     kv_load(0)
     kv_load(1)
 
-    barrier = pltpu.get_barrier_semaphore()
-    for dev in (left, right, peer):
-        pl.semaphore_signal(barrier, inc=1, device_id=to(dev), device_id_type=MESH)
     pl.semaphore_wait(barrier, 3)
 
     n_col = 2
@@ -378,28 +379,55 @@
     finish_gather(0, {})
     work = attn_steps(0) + [functools.partial(dx_chunk, 0, j) for j in range(rs_n)]
     later = [functools.partial(kv_total, 0)] + dw_steps(0)
-    for d, t, j in slots:
+    for i, (d, t, j) in enumerate(slots):
         ag_event(1, t, j, d)
+        if i == len(slots) - 2:
+            while work:
+                work.pop(0)()
+            for k in range(rs_n):
+                rs_start(0, k)
         (work or later).pop(0)()
+    finish_gather(1, {
+        (0, 1): [functools.partial(rs_event, 0, 0, half)],
+        (1, 0): [functools.partial(rs_event, 0, 1, half), functools.partial(rs_event, 0, 2, half)],
+        (1, 1): [functools.partial(rs_event, 0, 3, half)],
+    })
+    attn = attn_steps(1)
+    for k in range(heads):
+        attn.pop(0)()
+        rs_event(0, 2 * k, 3)
+        attn.pop(0)()
+        rs_event(0, 2 * k + 1, 3)
+    for f in attn:
+        f()
+    dx_chunk(1, 0)
+    dx_chunk(1, 1)
+    rs_event(0, 0, 2)
+    rs_start(1, 0)
+    dx_chunk(1, 2)
+    rs_event(0, 1, 2)
+    rs_start(1, 1)
+    dx_chunk(1, 3)
+    rs_event(0, 2, 2)
+    rs_start(1, 2)
+    later.pop(0)()
+    rs_event(0, 3, 2)
+    later.pop(0)()
+    rs_start(1, 3)
+    later += [functools.partial(kv_total, 1)] + dw_steps(1)
     for j in range(rs_n):
-        rs_start(0, j)
-    finish_gather(1, {})
-    work = attn_steps(1) + [functools.partial(dx_chunk, 1, j) for j in range(rs_n)]
-    for d in range(half, 1, -1):
-        for j in range(rs_n):
-            rs_event(0, j, d)
-            (work or later).pop(0)()
-    for j in range(rs_n):
-        rs_start(1, j)
-    later += [functools.partial(kv_total, 1)] + dw_steps(1)
+        later.pop(0)()
+        rs_event(1, j, half)
     for j in range(rs_n):
         rs_event(0, j, 1)
         later.pop(0)()
-    for d in range(half, 0, -1):
+    for d in range(half - 1, 0, -1):
         for j in range(rs_n):
             rs_event(1, j, d)
             if later:
                 later.pop(0)()
+    for f in later:
+        f()
 
     for m in range(micro_n):
         for t, j in tensor_cols:

time: 98.6 us -> 94.7 us (0.960)
  Pallas kernels: 97.7 us -> 93.8 us
    pallas_call x1, Pallas kernels: 92.7 us -> 88.8 us  [device_grads(): pl.pallas_call(functools.partial(attn_kernel, n_dev, kv_heads), out_shape...]
where the time goes in v4:
time: 94.7 us; the launch traced here: 94.6 us
  Pallas kernels  93.8 us (99%)
    pallas_call x1, Pallas kernels, device_grads(): pl.pallas_call(functools.partial(attn_kernel, n_dev, kv_heads), out_shape...  88.8 us
    pallas_call x1, Pallas kernels, device_grads(): pl.pallas_call(functools.partial(copy_kernel, len(grads)), out_shape=tupl...  5.03 us

profile of v4, /device:TPU:22, one launch (start us, length us, event | category | flops | bytes accessed | tf_op | source)
XLA Modules:
  0.0 94.6 jit_solution(129608351521616313)
XLA Ops:
  0.6 88.8 %shard_map.101 = (bf16[2,16,5120]{2,1,0:T(8,128)(2,1)S(1)}, f32[10240,128]{1,0:T(8,128)S(1)}, f32[2560,128]{1,0:T(8,128)S(1)}, f32[2560,128]{1,0:T(8,128)S(1)}, f32[256,5120]{1,0:T(8,128)S(1)}) custom-call(bf16[2,16,5120]{2,1,0:T(8,128)(2,1)} %x_in.1, bf16[2,16,5120]{2,1,0:T(8,128)(2,1)} %dy_in.1, bf16[10240,128]{1,0:T(8,128)(2,1)} %bitcast.8, ...), custom_call_target="tpu_custom_call" | custom-call | tf_op jit(solution)/shard_map/pallas_call | solution.py:504
  89.4 5.0 %shard_map.102 = (bf16[2,16,5120]{2,1,0:T(8,128)(2,1)}, f32[10240,128]{1,0:T(8,128)}, f32[2560,128]{1,0:T(8,128)}, f32[2560,128]{1,0:T(8,128)}, f32[256,5120]{1,0:T(8,128)}) custom-call(bf16[2,16,5120]{2,1,0:T(8,128)(2,1)S(1)} %get-tuple-element.15.refs_0_, f32[10240,128]{1,0:T(8,128)S(1)} %get-tuple-element.16.refs_1_, ...), custom_call_target="tpu_custom_call" | custom-call | tf_op jit(solution)/shard_map/pallas_call | solution.py:522

commit v5 on v4

--- a/solution.py
+++ b/solution.py
@@ -387,31 +387,41 @@
             for k in range(rs_n):
                 rs_start(0, k)
         (work or later).pop(0)()
-    finish_gather(1, {
-        (0, 1): [functools.partial(rs_event, 0, 0, half)],
-        (1, 0): [functools.partial(rs_event, 0, 1, half), functools.partial(rs_event, 0, 2, half)],
-        (1, 1): [functools.partial(rs_event, 0, 3, half)],
-    })
+    ev = functools.partial(rs_event, 0)
+    ag_event(1, 0, 0, half)
+    ag_event(1, 0, 1, half)
+    ag_event(1, 1, 0, half)
+    ev(0, half)
+    finish_part(1, 0, 0)
+    ev(1, half)
+    ev(2, half)
+    finish_part(1, 0, 1)
+    ev(3, half)
+    ag_event(1, 1, 1, half)
+    finish_part(1, 1, 0)
+    ev(0, half - 1)
+    finish_part(1, 1, 1)
+    ev(1, half - 1)
     attn = attn_steps(1)
-    for k in range(heads):
-        attn.pop(0)()
-        rs_event(0, 2 * k, 3)
-        attn.pop(0)()
-        rs_event(0, 2 * k + 1, 3)
+    attn.pop(0)()
+    ev(2, half - 1)
+    attn.pop(0)()
+    attn.pop(0)()
+    ev(3, half - 1)
     for f in attn:
         f()
+    ev(0, half - 2)
     dx_chunk(1, 0)
+    ev(1, half - 2)
     dx_chunk(1, 1)
-    rs_event(0, 0, 2)
+    ev(2, half - 2)
     rs_start(1, 0)
     dx_chunk(1, 2)
-    rs_event(0, 1, 2)
+    ev(3, half - 2)
     rs_start(1, 1)
     dx_chunk(1, 3)
-    rs_event(0, 2, 2)
     rs_start(1, 2)
     later.pop(0)()
-    rs_event(0, 3, 2)
     later.pop(0)()
     rs_start(1, 3)
     later += [functools.partial(kv_total, 1)] + dw_steps(1)
@@ -421,31 +431,42 @@
     for j in range(rs_n):
         rs_event(0, j, 1)
         later.pop(0)()
-    for d in range(half - 1, 0, -1):
+    for d in range(half - 1, 1, -1):
         for j in range(rs_n):
             rs_event(1, j, d)
             if later:
                 later.pop(0)()
     for f in later:
         f()
-
     for m in range(micro_n):
         for t, j in tensor_cols:
-            rows = n_chip - 1
-            ref = bufs[t][1].at[m, pl.ds(0, rows * tok), pl.ds(j * col_w, col_w)]
+            ref = bufs[t][1].at[m, pl.ds(0, (n_chip - 1) * tok), pl.ds(j * col_w, col_w)]
             pltpu.make_async_copy(ref, ref, ag_send.at[m, t, j]).wait()
             ref = peer_blocks(m, t, j, c)
             pltpu.make_async_copy(ref, ref, d2d_send.at[m, t, j]).wait()
         for j in range(rs_n):
             ref = psend.at[m, :, pl.ds(j * rs_w, rs_w)]
             pltpu.make_async_copy(ref, ref, ps_send.at[m, j]).wait()
+
+    def rs_drain(m):
+        for j in range(rs_n):
             ref = psend.at[m, pl.ds(0, (n_chip - 1) * tok), pl.ds(j * rs_w, rs_w)]
             pltpu.make_async_copy(ref, ref, rs_send.at[m, j]).wait()
 
+    rs_drain(0)
+    for j in range(rs_n):
+        rs_event(1, j, 1)
+    rs_drain(1)
+
 
 def copy_kernel(n, *refs):
     srcs, dsts, sem = refs[:n], refs[n:2 * n], refs[2 * n]
-    copies = [pltpu.make_async_copy(a, b, sem.at[i]) for i, (a, b) in enumerate(zip(srcs, dsts))]
+    pairs = []
+    for a, b in zip(srcs, dsts):
+        parts = max(1, a.shape[0] // 2560) if a.shape[-1] < 1024 else a.shape[0] // 64 or 1
+        rows = a.shape[0] // parts
+        pairs += [(a.at[pl.ds(i * rows, rows)], b.at[pl.ds(i * rows, rows)]) for i in range(parts)]
+    copies = [pltpu.make_async_copy(a, b, sem.at[i]) for i, (a, b) in enumerate(pairs)]
     for cp in copies:
         cp.start()
     for cp in copies:
@@ -524,7 +545,7 @@
             out_shape=tuple(jax.ShapeDtypeStruct(g.shape, g.dtype) for g in grads),
             in_specs=[pl.BlockSpec(memory_space=pltpu.VMEM)] * len(grads),
             out_specs=(any_spec,) * len(grads),
-            scratch_shapes=[dma((len(grads),))],
+            scratch_shapes=[dma((16,))],
             compiler_params=pltpu.CompilerParams(vmem_limit_bytes=1024 * 1024),
         )(*grads)
         return dx, dwq.reshape(d_model, heads, head_dim), dwk, dwv, dwo.reshape(heads, head_dim, d_model)

time: 94.7 us -> 95.9 us (1.013)
  Pallas kernels: 93.8 us -> 95 us
    pallas_call x1, Pallas kernels: 88.8 us -> 90.1 us  [device_grads(): pl.pallas_call(functools.partial(attn_kernel, n_dev, kv_heads), out_shape...]
where the time goes in v5:
time: 95.9 us; the launch traced here: 95.8 us
  Pallas kernels  95 us (99%)
    pallas_call x1, Pallas kernels, device_grads(): pl.pallas_call(functools.partial(attn_kernel, n_dev, kv_heads), out_shape...  90.1 us
    pallas_call x1, Pallas kernels, device_grads(): pl.pallas_call(functools.partial(copy_kernel, len(grads)), out_shape=tupl...  4.97 us

profile of v5, /device:TPU:22, one launch (start us, length us, event | category | flops | bytes accessed | tf_op | source)
XLA Modules:
  0.0 95.8 jit_solution(13946394776503562012)
XLA Ops:
  0.6 90.1 %shard_map.101 = (bf16[2,16,5120]{2,1,0:T(8,128)(2,1)S(1)}, f32[10240,128]{1,0:T(8,128)S(1)}, f32[2560,128]{1,0:T(8,128)S(1)}, f32[2560,128]{1,0:T(8,128)S(1)}, f32[256,5120]{1,0:T(8,128)S(1)}) custom-call(bf16[2,16,5120]{2,1,0:T(8,128)(2,1)} %x_in.1, bf16[2,16,5120]{2,1,0:T(8,128)(2,1)} %dy_in.1, bf16[10240,128]{1,0:T(8,128)(2,1)} %bitcast.8, ...), custom_call_target="tpu_custom_call" | custom-call | tf_op jit(solution)/shard_map/pallas_call | solution.py:525
  90.7 5.0 %shard_map.102 = (bf16[2,16,5120]{2,1,0:T(8,128)(2,1)}, f32[10240,128]{1,0:T(8,128)}, f32[2560,128]{1,0:T(8,128)}, f32[2560,128]{1,0:T(8,128)}, f32[256,5120]{1,0:T(8,128)}) custom-call(bf16[2,16,5120]{2,1,0:T(8,128)(2,1)S(1)} %get-tuple-element.15.refs_0_, f32[10240,128]{1,0:T(8,128)S(1)} %get-tuple-element.16.refs_1_, ...), custom_call_target="tpu_custom_call" | custom-call | tf_op jit(solution)/shard_map/pallas_call | solution.py:543

commit v6 on v5

--- a/solution.py
+++ b/solution.py
@@ -390,36 +390,32 @@
     ev = functools.partial(rs_event, 0)
     ag_event(1, 0, 0, half)
     ag_event(1, 0, 1, half)
+    finish_part(1, 0, 0)
     ag_event(1, 1, 0, half)
     ev(0, half)
-    finish_part(1, 0, 0)
+    finish_part(1, 0, 1)
     ev(1, half)
     ev(2, half)
-    finish_part(1, 0, 1)
+    finish_part(1, 1, 0)
+    ag_event(1, 1, 1, half)
     ev(3, half)
-    ag_event(1, 1, 1, half)
-    finish_part(1, 1, 0)
-    ev(0, half - 1)
     finish_part(1, 1, 1)
-    ev(1, half - 1)
     attn = attn_steps(1)
-    attn.pop(0)()
-    ev(2, half - 1)
-    attn.pop(0)()
-    attn.pop(0)()
-    ev(3, half - 1)
+    for k in range(2 * heads):
+        ev(k, half - 1)
+        attn.pop(0)()
     for f in attn:
         f()
+    dx_chunk(1, 0)
     ev(0, half - 2)
-    dx_chunk(1, 0)
+    dx_chunk(1, 1)
     ev(1, half - 2)
-    dx_chunk(1, 1)
-    ev(2, half - 2)
     rs_start(1, 0)
     dx_chunk(1, 2)
-    ev(3, half - 2)
+    ev(2, half - 2)
     rs_start(1, 1)
     dx_chunk(1, 3)
+    ev(3, half - 2)
     rs_start(1, 2)
     later.pop(0)()
     later.pop(0)()

time: 95.9 us -> 95.1 us (level)
  no operation moved by 1% of the time
where the time goes in v6:
time: 95.1 us
  Pallas kernels  94.3 us (99%)
    pallas_call x1, Pallas kernels, device_grads(): pl.pallas_call(functools.partial(attn_kernel, n_dev, kv_heads), out_shape...  89.3 us
    pallas_call x1, Pallas kernels, device_grads(): pl.pallas_call(functools.partial(copy_kernel, len(grads)), out_shape=tupl...  4.97 us

profile of v6, /device:TPU:22, one launch (start us, length us, event | category | flops | bytes accessed | tf_op | source)
XLA Modules:
  0.0 95.1 jit_solution(10957262037014203094)
XLA Ops:
  0.6 89.3 %shard_map.101 = (bf16[2,16,5120]{2,1,0:T(8,128)(2,1)S(1)}, f32[10240,128]{1,0:T(8,128)S(1)}, f32[2560,128]{1,0:T(8,128)S(1)}, f32[2560,128]{1,0:T(8,128)S(1)}, f32[256,5120]{1,0:T(8,128)S(1)}) custom-call(bf16[2,16,5120]{2,1,0:T(8,128)(2,1)} %x_in.1, bf16[2,16,5120]{2,1,0:T(8,128)(2,1)} %dy_in.1, bf16[10240,128]{1,0:T(8,128)(2,1)} %bitcast.8, ...), custom_call_target="tpu_custom_call" | custom-call | tf_op jit(solution)/shard_map/pallas_call | solution.py:521
  89.9 5.0 %shard_map.102 = (bf16[2,16,5120]{2,1,0:T(8,128)(2,1)}, f32[10240,128]{1,0:T(8,128)}, f32[2560,128]{1,0:T(8,128)}, f32[2560,128]{1,0:T(8,128)}, f32[256,5120]{1,0:T(8,128)}) custom-call(bf16[2,16,5120]{2,1,0:T(8,128)(2,1)S(1)} %get-tuple-element.15.refs_0_, f32[10240,128]{1,0:T(8,128)S(1)} %get-tuple-element.16.refs_1_, ...), custom_call_target="tpu_custom_call" | custom-call | tf_op jit(solution)/shard_map/pallas_call | solution.py:539

commit v7 on v6

--- a/solution.py
+++ b/solution.py
@@ -390,48 +390,51 @@
     ev = functools.partial(rs_event, 0)
     ag_event(1, 0, 0, half)
     ag_event(1, 0, 1, half)
+    ev(0, half)
     finish_part(1, 0, 0)
     ag_event(1, 1, 0, half)
-    ev(0, half)
-    finish_part(1, 0, 1)
     ev(1, half)
     ev(2, half)
-    finish_part(1, 1, 0)
+    finish_part(1, 0, 1)
     ag_event(1, 1, 1, half)
     ev(3, half)
+    finish_part(1, 1, 0)
     finish_part(1, 1, 1)
     attn = attn_steps(1)
     for k in range(2 * heads):
+        attn.pop(0)()
         ev(k, half - 1)
-        attn.pop(0)()
     for f in attn:
         f()
     dx_chunk(1, 0)
+    dx_chunk(1, 1)
     ev(0, half - 2)
-    dx_chunk(1, 1)
-    ev(1, half - 2)
     rs_start(1, 0)
     dx_chunk(1, 2)
-    ev(2, half - 2)
+    ev(1, half - 2)
     rs_start(1, 1)
     dx_chunk(1, 3)
-    ev(3, half - 2)
+    ev(2, half - 2)
     rs_start(1, 2)
     later.pop(0)()
+    ev(3, half - 2)
     later.pop(0)()
     rs_start(1, 3)
     later += [functools.partial(kv_total, 1)] + dw_steps(1)
     for j in range(rs_n):
-        later.pop(0)()
+        if j < rs_n - 1:
+            later.pop(0)()
         rs_event(1, j, half)
     for j in range(rs_n):
+        rs_event(1, j, half - 1)
+        later.pop(0)()
+    for j in range(rs_n):
         rs_event(0, j, 1)
-        later.pop(0)()
-    for d in range(half - 1, 1, -1):
-        for j in range(rs_n):
-            rs_event(1, j, d)
-            if later:
-                later.pop(0)()
+        if later:
+            later.pop(0)()
+        rs_event(1, j, half - 2)
+        if later:
+            later.pop(0)()
     for f in later:
         f()
     for m in range(micro_n):

time: 95.1 us -> 94.6 us (level)
  no operation moved by 1% of the time
where the time goes in v7:
time: 94.6 us; the launch traced here: 94.5 us
  Pallas kernels  93.7 us (99%)
    pallas_call x1, Pallas kernels, device_grads(): pl.pallas_call(functools.partial(attn_kernel, n_dev, kv_heads), out_shape...  88.8 us
    pallas_call x1, Pallas kernels, device_grads(): pl.pallas_call(functools.partial(copy_kernel, len(grads)), out_shape=tupl...  4.97 us

profile of v7, /device:TPU:22, one launch (start us, length us, event | category | flops | bytes accessed | tf_op | source)
XLA Modules:
  0.0 94.5 jit_solution(12765343047677630862)
XLA Ops:
  0.6 88.8 %shard_map.101 = (bf16[2,16,5120]{2,1,0:T(8,128)(2,1)S(1)}, f32[10240,128]{1,0:T(8,128)S(1)}, f32[2560,128]{1,0:T(8,128)S(1)}, f32[2560,128]{1,0:T(8,128)S(1)}, f32[256,5120]{1,0:T(8,128)S(1)}) custom-call(bf16[2,16,5120]{2,1,0:T(8,128)(2,1)} %x_in.1, bf16[2,16,5120]{2,1,0:T(8,128)(2,1)} %dy_in.1, bf16[10240,128]{1,0:T(8,128)(2,1)} %bitcast.8, ...), custom_call_target="tpu_custom_call" | custom-call | tf_op jit(solution)/shard_map/pallas_call | solution.py:524
  89.4 5.0 %shard_map.102 = (bf16[2,16,5120]{2,1,0:T(8,128)(2,1)}, f32[10240,128]{1,0:T(8,128)}, f32[2560,128]{1,0:T(8,128)}, f32[2560,128]{1,0:T(8,128)}, f32[256,5120]{1,0:T(8,128)}) custom-call(bf16[2,16,5120]{2,1,0:T(8,128)(2,1)S(1)} %get-tuple-element.15.refs_0_, f32[10240,128]{1,0:T(8,128)S(1)} %get-tuple-element.16.refs_1_, ...), custom_call_target="tpu_custom_call" | custom-call | tf_op jit(solution)/shard_map/pallas_call | solution.py:542

commit v8 on v7

--- a/solution.py
+++ b/solution.py
@@ -22,10 +22,10 @@
 
 def attn_kernel(n_dev, kv_heads, x_in, dy_in, wq_in, wk_in, wv_in, wo_in,
                 dx_own, dwq, dwk, dwv, dwo,
-                xb, dyb, wq, wo, wkv, stage_q, stage_kv, unpacked,
-                acc_q, acc_kv, acc_do, qb, kvb, dob, ob, dqb, dkvp, prob_b, ds_b,
+                xb, dyb, wall, wo, stage_q, stage_kv, unpacked,
+                acc_x, acc_do, qb, kvb, dob, ob, dqb, dkvp, prob_b, ds_b,
                 dkv_f, dkv_peer, dkv_tot,
-                dx_f, dx_tmp, psend, precv, sbuf, rbuf,
+                dx_f, psend, precv, sbuf, rbuf,
                 own_sem, w_sem, kvw_sem,
                 ag_send, ag_recv, d2d_send, d2d_recv, wx_sem,
                 dkv_sem, ps_send, ps_recv, rs_send, rs_recv):
@@ -33,7 +33,8 @@
     half = n_chip // 2
     micro_n, tok, d_model = x_in.shape
     head_dim = wk_in.shape[1]
-    heads = wq.shape[1] // head_dim
+    hd = wo.shape[0]
+    heads = hd // head_dim
     n_rows = n_dev * tok
     par_rows = n_rows // 2
     me = lax.axis_index("model")
@@ -135,13 +136,13 @@
         def body(i, _):
             unpacked[...] = stage_q[pl.ds(pl.multiple_of(i * un_rows, un_rows), un_rows), :].astype(F32)
             for h in range(heads):
-                wq[pl.ds(pl.multiple_of(i * per, per), per), h * head_dim:(h + 1) * head_dim] = (
+                wall[pl.ds(pl.multiple_of(i * per, per), per), h * head_dim:(h + 1) * head_dim] = (
                     unpacked[pl.ds(h, per, stride=heads), :].astype(BF16))
             return 0
 
         lax.fori_loop(0, stage_q.shape[0] // un_rows, body, 0)
 
-    kv_col = pl.multiple_of(c * head_dim, head_dim)
+    kv_col = pl.multiple_of(hd + c * head_dim, head_dim)
 
     def prep_kv(i):
         pltpu.make_async_copy(wk_in.at[pl.ds(i * kv_rows, kv_rows)], stage_kv.at[i % 2], kvw_sem.at[i % 2]).wait()
@@ -150,7 +151,7 @@
 
         def body(k, _):
             unpacked[...] = stage_kv[i % 2, pl.ds(pl.multiple_of(k * un_rows, un_rows), un_rows), :].astype(F32)
-            wkv[pl.ds(pl.multiple_of(base + k * per, per), per), pl.ds(kv_col, head_dim)] = (
+            wall[pl.ds(pl.multiple_of(base + k * per, per), per), pl.ds(kv_col, head_dim)] = (
                 unpacked[pl.ds(z, per, stride=kv_heads), :].astype(BF16))
             return 0
 
@@ -159,27 +160,24 @@
             kv_load(i + 2)
 
     def kv_swap():
-        ref = wkv.at[:, pl.ds(kv_col, head_dim)]
+        ref = wall.at[:, pl.ds(kv_col, head_dim)]
         pltpu.make_async_remote_copy(src_ref=ref, dst_ref=ref, send_sem=wx_sem.at[0], recv_sem=wx_sem.at[1],
                                      device_id=to(peer), device_id_type=MESH).start()
 
     def kv_swap_wait():
-        ref = wkv.at[:, pl.ds(kv_col, head_dim)]
+        ref = wall.at[:, pl.ds(kv_col, head_dim)]
         pltpu.make_async_copy(ref, ref, wx_sem.at[0]).wait()
-        ref = wkv.at[:, pl.ds(pl.multiple_of((1 - c) * head_dim, head_dim), head_dim)]
+        ref = wall.at[:, pl.ds(pl.multiple_of(hd + (1 - c) * head_dim, head_dim), head_dim)]
         pltpu.make_async_copy(ref, ref, wx_sem.at[1]).wait()
 
     def proj_x(m, j):
         for k in range(2):
             cols = slice(j * col_w + k * sub_w, j * col_w + (k + 1) * sub_w)
-            a = dot(xb[m, :, cols], wq[cols, :])
-            b = dot(xb[m, :, cols], wkv[cols, :])
+            a = dot(xb[m, :, cols], wall[cols, :])
             if j == 0 and k == 0:
-                acc_q[...] = a
-                acc_kv[...] = b
+                acc_x[...] = a
             else:
-                acc_q[...] += a
-                acc_kv[...] += b
+                acc_x[...] += a
 
     def proj_dy(m, j):
         for k in range(2):
@@ -191,8 +189,8 @@
                 acc_do[...] += a
 
     def round_x():
-        qb[...] = acc_q[...].astype(BF16)
-        kvb[...] = acc_kv[...].astype(BF16)
+        qb[...] = acc_x[:, :hd].astype(BF16)
+        kvb[...] = acc_x[:, hd:].astype(BF16)
 
     def round_dy():
         dob[...] = acc_do[...].astype(BF16)
@@ -278,11 +276,12 @@
 
     def dx_chunk(m, j):
         cols = slice(j * rs_w, (j + 1) * rs_w)
-        dx_tmp[...] = dot(dqb[m], wq[cols, :], NT) + dot(dkvp[...], wkv[cols, :], NT)
         away = pl.ds(pl.multiple_of((1 - c) * par_rows, par_rows), par_rows)
         keep = pl.ds(pl.multiple_of(c * par_rows, par_rows), par_rows)
-        psend[m, :, cols] = dx_tmp[away, :].astype(BF16)
-        dx_f[m, :, cols] = dx_tmp[keep, :]
+        lhs = jnp.concatenate([jnp.concatenate([dqb[m, rows, :], dkvp[rows, :]], axis=1) for rows in (away, keep)], axis=0)
+        part = dot(lhs, wall[cols, :], NT)
+        psend[m, :, cols] = part[:par_rows].astype(BF16)
+        dx_f[m, :, cols] = part[par_rows:]
         pltpu.make_async_remote_copy(src_ref=psend.at[m, :, cols], dst_ref=precv.at[m, :, cols],
                                      send_sem=ps_send.at[m, j], recv_sem=ps_recv.at[m, j],
                                      device_id=to(peer), device_id_type=MESH).start()
@@ -489,14 +488,12 @@
         scratch = [
             pltpu.VMEM((micro_n, n_rows, d_model), BF16),
             pltpu.VMEM((micro_n, n_rows, d_model), BF16),
-            pltpu.VMEM((d_model, hd), BF16),
+            pltpu.VMEM((d_model, hd + 2 * head_dim), BF16),
             pltpu.VMEM((hd, d_model), BF16),
-            pltpu.VMEM((d_model, 2 * head_dim), BF16),
             pltpu.VMEM((d_model * heads, head_dim), BF16),
             pltpu.VMEM((2, d_model * kv_heads // 8, head_dim), BF16),
             pltpu.VMEM((512, head_dim), F32),
-            pltpu.VMEM((n_rows, hd), F32),
-            pltpu.VMEM((n_rows, 2 * head_dim), F32),
+            pltpu.VMEM((n_rows, hd + 2 * head_dim), F32),
             pltpu.VMEM((n_rows, hd), F32),
             pltpu.VMEM((n_rows, hd), BF16),
             pltpu.VMEM((n_rows, 2 * head_dim), BF16),
@@ -510,7 +507,6 @@
             pltpu.VMEM((micro_n, n_rows, 2 * head_dim), F32),
             pltpu.VMEM((micro_n, n_rows, 2 * head_dim), BF16),
             pltpu.VMEM((micro_n, par_rows, d_model), F32),
-            pltpu.VMEM((n_rows, d_model // 4), F32),
             pltpu.VMEM((micro_n, par_rows, d_model), BF16),
             pltpu.VMEM((micro_n, par_rows, d_model), BF16),
             pltpu.VMEM((micro_n, 2, half, tok, d_model), BF16),

time: 94.6 us -> 94.2 us (level)
  no operation moved by 1% of the time
where the time goes in v8:
time: 94.2 us; the launch traced here: 94.1 us
  Pallas kernels  93.3 us (99%)
    pallas_call x1, Pallas kernels, device_grads(): pl.pallas_call(functools.partial(attn_kernel, n_dev, kv_heads), out_shape...  88.3 us
    pallas_call x1, Pallas kernels, device_grads(): pl.pallas_call(functools.partial(copy_kernel, len(grads)), out_shape=tupl...  4.97 us

profile of v8, /device:TPU:22, one launch (start us, length us, event | category | flops | bytes accessed | tf_op | source)
XLA Modules:
  0.0 94.1 jit_solution(596947431539145069)
XLA Ops:
  0.6 88.3 %shard_map.101 = (bf16[2,16,5120]{2,1,0:T(8,128)(2,1)S(1)}, f32[10240,128]{1,0:T(8,128)S(1)}, f32[2560,128]{1,0:T(8,128)S(1)}, f32[2560,128]{1,0:T(8,128)S(1)}, f32[256,5120]{1,0:T(8,128)S(1)}) custom-call(bf16[2,16,5120]{2,1,0:T(8,128)(2,1)} %x_in.1, bf16[2,16,5120]{2,1,0:T(8,128)(2,1)} %dy_in.1, bf16[10240,128]{1,0:T(8,128)(2,1)} %bitcast.8, ...), custom_call_target="tpu_custom_call" | custom-call | tf_op jit(solution)/shard_map/pallas_call | solution.py:520
  89.0 5.0 %shard_map.102 = (bf16[2,16,5120]{2,1,0:T(8,128)(2,1)}, f32[10240,128]{1,0:T(8,128)}, f32[2560,128]{1,0:T(8,128)}, f32[2560,128]{1,0:T(8,128)}, f32[256,5120]{1,0:T(8,128)}) custom-call(bf16[2,16,5120]{2,1,0:T(8,128)(2,1)S(1)} %get-tuple-element.15.refs_0_, f32[10240,128]{1,0:T(8,128)S(1)} %get-tuple-element.16.refs_1_, ...), custom_call_target="tpu_custom_call" | custom-call | tf_op jit(solution)/shard_map/pallas_call | solution.py:538

commit v9 on v8

--- a/solution.py
+++ b/solution.py
@@ -389,8 +389,8 @@
     ev = functools.partial(rs_event, 0)
     ag_event(1, 0, 0, half)
     ag_event(1, 0, 1, half)
+    finish_part(1, 0, 0)
     ev(0, half)
-    finish_part(1, 0, 0)
     ag_event(1, 1, 0, half)
     ev(1, half)
     ev(2, half)

time: 94.2 us -> 94.2 us (level)
  no operation moved by 1% of the time
where the time goes in v9:
time: 94.2 us; the launch traced here: 94.1 us
  Pallas kernels  93.3 us (99%)
    pallas_call x1, Pallas kernels, device_grads(): pl.pallas_call(functools.partial(attn_kernel, n_dev, kv_heads), out_shape...  88.4 us
    pallas_call x1, Pallas kernels, device_grads(): pl.pallas_call(functools.partial(copy_kernel, len(grads)), out_shape=tupl...  4.97 us

profile of v9, /device:TPU:22, one launch (start us, length us, event | category | flops | bytes accessed | tf_op | source)
XLA Modules:
  0.0 94.1 jit_solution(11516105929034602857)
XLA Ops:
  0.6 88.4 %shard_map.101 = (bf16[2,16,5120]{2,1,0:T(8,128)(2,1)S(1)}, f32[10240,128]{1,0:T(8,128)S(1)}, f32[2560,128]{1,0:T(8,128)S(1)}, f32[2560,128]{1,0:T(8,128)S(1)}, f32[256,5120]{1,0:T(8,128)S(1)}) custom-call(bf16[2,16,5120]{2,1,0:T(8,128)(2,1)} %x_in.1, bf16[2,16,5120]{2,1,0:T(8,128)(2,1)} %dy_in.1, bf16[10240,128]{1,0:T(8,128)(2,1)} %bitcast.8, ...), custom_call_target="tpu_custom_call" | custom-call | tf_op jit(solution)/shard_map/pallas_call | solution.py:520
  89.0 5.0 %shard_map.102 = (bf16[2,16,5120]{2,1,0:T(8,128)(2,1)}, f32[10240,128]{1,0:T(8,128)}, f32[2560,128]{1,0:T(8,128)}, f32[2560,128]{1,0:T(8,128)}, f32[256,5120]{1,0:T(8,128)}) custom-call(bf16[2,16,5120]{2,1,0:T(8,128)(2,1)S(1)} %get-tuple-element.15.refs_0_, f32[10240,128]{1,0:T(8,128)S(1)} %get-tuple-element.16.refs_1_, ...), custom_call_target="tpu_custom_call" | custom-call | tf_op jit(solution)/shard_map/pallas_call | solution.py:538
